TPU v7x, 512 devices: a whole 4x8x8 slice. The times are simulated.
512 devices in a mesh: dp: 32 (over x, y), tensor: 16 (over z, core).
Axes of the slice: x: 4, y: 8, z: 8, core: 2. Of those that a mesh axis runs over, the one named last changes fastest.
Arguments:
- queries: bfloat16 [4096, 16384], P('dp', 'tensor'), may hold values from -24 to 24
- draft_keys: bfloat16 [4096, 1024], P('dp'), may hold values from -6 to 6
- draft_values: bfloat16 [4096, 1024], P('dp'), may hold values from -6 to 6
- cache_keys: bfloat16 [64, 2048, 1024], P('dp', 'tensor'), may hold values from -24 to 24
- cache_values: bfloat16 [64, 2048, 1024], P('dp', 'tensor'), may hold values from -6 to 6
- out_weight: bfloat16 [16384, 16384], P('tensor', 'dp'), may hold values from -0.25 to 0.25
- cache_lengths: int32 [64], P('dp'), may hold values from 512 to 2048
- draft_lengths: int32 [64], replicated, may hold values from 8 to 64
- dest_group: int32 [64], replicated, may hold values from 0 to 31, as said below
- dest_offset: int32 [64], replicated, may hold values from 0 to 32, as said below
Outputs:
- verified: bfloat16 [3072, 16384], P('tensor', 'dp')
Inputs may be any that keep to these rules, and one draw needn't show every extreme that they name: `dest_group`: at most one request of a group has another group as destination, and each group receives at most one such request. `dest_offset`: blocks with the same destination never intersect and end at packed row 96 or before; a block moved to another group starts right after that group's own rows; in every draw some group's blocks fill all 96 rows.
All inputs are finite; a program needn't handle non-finite values.
Results may differ from a plain program's by a relative error of at most 0.017.
Values may be sent and summed in bfloat16 or wider, within the bound.
No kernel may reach another device: no remote copies, remote signals or barrier semaphores. Data moves between devices by JAX's collectives and lax.ppermute only.
A program may use at most 64 MiB of HBM per device.

v0:
```python
import jax
import jax.numpy as jnp
from jax import lax
from jax.experimental import pallas as pl
from jax.experimental.pallas import tpu as pltpu
from jax.sharding import Mesh, PartitionSpec as P


HEAD_DIM = 128
DRAFT = 64
PACK = 96
REQUESTS = 64
NX, NY, NZ = 4, 8, 8
NEG_FILL = -1e30
BF16 = jnp.bfloat16
F32 = jnp.float32
NT = (((1,), (1,)), ((), ()))
VMEM = pl.BlockSpec(memory_space=pltpu.VMEM)
SMEM = pl.BlockSpec(memory_space=pltpu.SMEM)
ANY = pl.BlockSpec(memory_space=pl.ANY)
TOKEN = jax.ShapeDtypeStruct((8, 128), F32)

CHUNKS = ((0, -1, 1), (-2, 2), (-3, 3, -4))


def shift(value, axis, size, step):
    return lax.ppermute(value, axis, [(i, (i + step) % size) for i in range(size)])


def kv_kernel(k_ref, v_ref, o_ref):
    for h in range(NZ):
        o_ref[h, 0, 0] = k_ref[0, :, h * HEAD_DIM : (h + 1) * HEAD_DIM]
        o_ref[h, 0, 1] = v_ref[0, :, h * HEAD_DIM : (h + 1) * HEAD_DIM]


def pack_kv(k, v):
    return pl.pallas_call(
        kv_kernel,
        grid=(2,),
        in_specs=[pl.BlockSpec((1, 128, 1024), lambda r: (r, 0, 0))] * 2,
        out_specs=pl.BlockSpec((NZ, 1, 2, 128, 128), lambda r: (0, r, 0, 0, 0)),
        out_shape=jax.ShapeDtypeStruct((NZ, 2, 2, 128, 128), BF16),
        name="pack_kv",
    )(k, v)


def transpose_kernel(w_ref, o_ref):
    o_ref[...] = w_ref[...].T


def transpose(w):
    return pl.pallas_call(
        transpose_kernel,
        grid=(4,),
        in_specs=[pl.BlockSpec((1024, 128), lambda i: (0, i))],
        out_specs=pl.BlockSpec((128, 1024), lambda i: (i, 0)),
        out_shape=jax.ShapeDtypeStruct((512, 1024), BF16),
        name="transpose_w",
    )(w)


def attend_kernel(s_ref, mine_ref, other_ref, kv_ref, dk_ref, dv_ref, o_ref):
    cache_len = s_ref[2]
    draft_len = s_ref[3]
    scale = HEAD_DIM ** (-0.5)
    keys = kv_ref[:, 0].reshape(2048, HEAD_DIM)
    values = kv_ref[:, 1].reshape(2048, HEAD_DIM)
    dk = dk_ref[...]
    dv = dv_ref[...]
    keep = lax.broadcasted_iota(jnp.int32, (1, 2048), 1) < cache_len
    row = lax.broadcasted_iota(jnp.int32, (128, DRAFT), 0) % DRAFT
    slot = lax.broadcasted_iota(jnp.int32, (128, DRAFT), 1)
    keep_draft = (slot <= row) & (slot < draft_len)
    live = lax.broadcasted_iota(jnp.int32, (128, 1), 0) % DRAFT < draft_len
    for side, q_ref in enumerate((mine_ref, other_ref)):
        q = jnp.concatenate([q_ref[:, :HEAD_DIM], q_ref[:, HEAD_DIM:]], axis=0)
        cached = lax.dot_general(q, keys, NT, preferred_element_type=F32) * scale
        drafted = lax.dot_general(q, dk, NT, preferred_element_type=F32) * scale
        cached = jnp.where(keep, cached, NEG_FILL)
        drafted = jnp.where(keep_draft, drafted, NEG_FILL)
        high = jnp.maximum(
            jnp.max(cached, axis=1, keepdims=True), jnp.max(drafted, axis=1, keepdims=True)
        )
        cached = jnp.exp(cached - high)
        drafted = jnp.exp(drafted - high)
        total = jnp.sum(cached, axis=1, keepdims=True) + jnp.sum(drafted, axis=1, keepdims=True)
        mixed = jnp.dot(cached.astype(BF16), values, preferred_element_type=F32)
        mixed = mixed + jnp.dot(drafted.astype(BF16), dv, preferred_element_type=F32)
        mixed = jnp.where(live, mixed / total, 0.0).astype(BF16)
        o_ref[side, :, :HEAD_DIM] = mixed[:DRAFT]
        o_ref[side, :, HEAD_DIM:] = mixed[DRAFT:]


def attend(scalars, q, other_q, kv, dk, dv):
    draft = pl.BlockSpec((DRAFT, HEAD_DIM), lambda p, s: (s[1], s[0]))
    return pl.pallas_call(
        attend_kernel,
        grid_spec=pltpu.PrefetchScalarGridSpec(
            num_scalar_prefetch=1,
            grid=(4,),
            in_specs=[
                pl.BlockSpec((DRAFT, 256), lambda p, s: (s[1], p)),
                pl.BlockSpec((DRAFT, 256), lambda p, s: (0, p)),
                pl.BlockSpec((16, 2, 128, 128), lambda p, s: (0, 0, 0, 0)),
                draft,
                draft,
            ],
            out_specs=pl.BlockSpec((2, DRAFT, 256), lambda p, s: (0, 0, p)),
        ),
        out_shape=jax.ShapeDtypeStruct((2, DRAFT, 1024), BF16),
        name="attend",
    )(scalars, q, other_q, kv, dk, dv)


def project_kernel(count, s_ref, *refs):
    rows, own, far = refs[:count], refs[count : count + 4], refs[count + 4 : count + 8]
    o_ref, token_ref = refs[-2:]
    token_ref[...] = jnp.zeros(token_ref.shape, F32)
    x = s_ref[0]
    width = count * DRAFT
    a = jnp.concatenate([ref[0] for ref in rows], axis=0)
    b = jnp.concatenate([ref[1] for ref in rows], axis=0)
    for step, own_ref, far_ref in zip((0, -1, 1, 2), own, far):
        acc = lax.dot_general(own_ref[...], a, NT, preferred_element_type=F32)
        acc = acc + lax.dot_general(far_ref[...], b, NT, preferred_element_type=F32)
        acc = acc.astype(BF16).reshape(NZ, 2, 32, width)
        at = lax.rem(x + step + NX, NX)
        for half in range(2):
            o_ref[at, :, :, half * width : (half + 1) * width] = acc[:, half]


def project(x, rows, own, far, token):
    count = len(rows)
    return pl.pallas_call(
        lambda *refs: project_kernel(count, *refs),
        in_specs=[SMEM] + [VMEM] * (count + 8) + [ANY],
        out_specs=[VMEM, VMEM],
        out_shape=[jax.ShapeDtypeStruct((NX, NZ, 32, 2 * count * DRAFT), BF16), TOKEN],
        name="project",
    )(x, *rows, *own, *far, token)


def place_kernel(s_ref, *refs):
    parts, o_ref, f_ref = refs[:-2], refs[-2], refs[-1]
    f_ref[...] = jnp.zeros(f_ref.shape, F32)
    my_y = s_ref[3 * REQUESTS]
    core = s_ref[3 * REQUESTS + 1]
    lane = lax.broadcasted_iota(jnp.int32, (32, 128), 1)
    for x in range(NX):
        for slots, ref in zip(CHUNKS, parts):
            width = len(slots) * DRAFT
            for tile in range(2 * width // 128):
                slab = ref[x, 0, :, tile * 128 : (tile + 1) * 128].astype(F32)
                for z in range(1, NZ):
                    slab = slab + ref[x, z, :, tile * 128 : (tile + 1) * 128].astype(F32)
                for part in range(2):
                    column, at = divmod(2 * tile + part, len(slots))
                    request = (x * NY + lax.rem(my_y + slots[at] + NY, NY)) * 2 + core
                    length = s_ref[request]
                    group = s_ref[REQUESTS + request]
                    first = s_ref[2 * REQUESTS + request]
                    moved = pltpu.roll(slab, lax.rem(first + 64 * part, 128), 1)
                    keep = (lane >= first) & (lane < first + length)
                    spot = 2 * group + column
                    f_ref[spot] = f_ref[spot] + jnp.where(keep, moved, 0.0)
    for t in range(16):
        a, b, c, d = (f_ref[4 * t + i] for i in range(4))
        b, c, d = pltpu.roll(b, 96, 1), pltpu.roll(c, 64, 1), pltpu.roll(d, 32, 1)
        o_ref[t, :, :128] = jnp.where(lane < 96, a, b).astype(BF16)
        o_ref[t, :, 128:256] = jnp.where(lane < 64, b, c).astype(BF16)
        o_ref[t, :, 256:] = jnp.where(lane < 32, c, d).astype(BF16)


def place(scalars, parts):
    return pl.pallas_call(
        place_kernel,
        in_specs=[SMEM] + [VMEM] * len(parts),
        out_specs=VMEM,
        out_shape=jax.ShapeDtypeStruct((16, 32, 4 * PACK), BF16),
        scratch_shapes=[pltpu.VMEM((64, 32, 128), F32)],
        name="place",
    )(scalars, *parts)


def finish_kernel(i_ref, o_ref):
    lane = lax.broadcasted_iota(jnp.int32, (32, 128), 1)
    blocks = [[], []]
    for z in range(NZ):
        v = i_ref[2 * z].astype(F32) + i_ref[2 * z + 1].astype(F32)
        v = [v[:, i * 128 : (i + 1) * 128] for i in range(3)]
        blocks[0].append(v[0])
        blocks[0].append(pltpu.roll(jnp.where(lane < 64, v[1], v[0]), 32, 1))
        blocks[1].append(pltpu.roll(jnp.where(lane < 32, v[2], v[1]), 64, 1))
        blocks[1].append(pltpu.roll(v[2], 96, 1))
    for g in range(2):
        block = jnp.concatenate(blocks[g], axis=0).astype(BF16).T
        o_ref[g * PACK : (g + 1) * PACK] = block[:PACK]


def finish(parts):
    return pl.pallas_call(
        finish_kernel,
        in_specs=[VMEM],
        out_specs=VMEM,
        out_shape=jax.ShapeDtypeStruct((2 * PACK, 512), BF16),
        name="finish",
    )(parts)


def exchange(value, axes):
    return lax.all_to_all(value, axes, 0, 0, tiled=True)


def layer(
    queries,
    draft_keys,
    draft_values,
    cache_keys,
    cache_values,
    out_weight,
    cache_lengths,
    draft_lengths,
    dest_group,
    dest_offset,
):
    x, y, z, c = (lax.axis_index(name).astype(jnp.int32) for name in ("x", "y", "z", "c"))
    request = (x * NY + y) * 2 + c
    cache_length = lax.dynamic_slice_in_dim(cache_lengths, c, 1)
    draft_length = lax.dynamic_slice_in_dim(draft_lengths, request, 1)
    scalars = jnp.concatenate([jnp.stack([z, c]), cache_length, draft_length])
    table = jnp.concatenate([draft_lengths, dest_group, dest_offset, jnp.stack([y, c])])

    kv = exchange(pack_kv(cache_keys, cache_values).reshape(16, 2, 128, 128), ("z", "c"))

    w0 = transpose(out_weight)
    w1, w2 = shift(w0, "x", NX, 1), shift(w0, "x", NX, -1)
    w3 = jnp.concatenate([shift(w1[:256], "x", NX, 1), shift(w2[256:], "x", NX, -1)], axis=0)
    own = [w0, w1, w2, w3]
    far = [shift(w, "c", 2, 1) for w in own]
    other_q = lax.dynamic_slice_in_dim(queries, (1 - c) * DRAFT, DRAFT, 0)
    other_q = shift(other_q, "c", 2, 1)

    rows = attend(scalars, queries, other_q, kv, draft_keys, draft_values)
    up1, down1 = shift(rows, "y", NY, 1), shift(rows, "y", NY, -1)
    up2, down2 = shift(rows, "y", NY, 2), shift(rows, "y", NY, -2)
    up3, down3 = shift(up2, "y", NY, 1), shift(down2, "y", NY, -1)
    up4, down4 = shift(up2[:1], "y", NY, 2), shift(down2[1:], "y", NY, -2)
    arrived = {0: rows, -1: up1, 1: down1, -2: up2, 2: down2, -3: up3, 3: down3}
    arrived[-4] = jnp.concatenate([up4, down4], axis=0)

    token = jnp.zeros(TOKEN.shape, F32)
    sums = []
    for slots in CHUNKS:
        part, token = project(x[None], [arrived[s] for s in slots], own, far, token)
        part = part.reshape(NX * NZ, 32, -1)
        sums.append(exchange(part, ("x", "z")).reshape(NX, NZ, 32, -1))
    return finish(exchange(place(table, sums), ("z", "c")))


def solution(mesh):
    fine = Mesh(mesh.devices.reshape(NX, NY, NZ, 2), ("x", "y", "z", "c"))
    xy, zc = ("x", "y"), ("z", "c")
    in_specs = (
        P(xy, zc),
        P(xy, None),
        P(xy, None),
        P(xy, zc, None),
        P(xy, zc, None),
        P(zc, xy),
        P(xy),
        P(),
        P(),
        P(),
    )
    return jax.shard_map(layer, mesh=fine, in_specs=in_specs, out_specs=P(zc, xy), check_vma=False)
```

profile of v0, /device:TPU:1, one launch (start us, length us, event | category | flops | bytes accessed | tf_op | source)
XLA Modules:
  0.0 224.2 jit_solution(2699702468417569861)
XLA Ops:
  0.0 3.6 %transpose_w.1.refs_4_.refs_3_ = bf16[512,1024]{1,0:T(8,128)(2,1)} custom-call(bf16[1024,512]{1,0:T(8,128)(2,1)} %w_ref.1), custom_call_target="tpu_custom_call" | custom-call | tf_op jit(solution)/shard_map/transpose_w/pallas_call | solution.py:52
  3.6 3.9 %collective-permute-start.3 = (bf16[512,1024]{1,0:T(8,128)(2,1)}, bf16[512,1024]{1,0:T(8,128)(2,1)S(1)}, u32[]{:S(2)}, u32[]{:S(2)}) collective-permute-start(bf16[512,1024]{1,0:T(8,128)(2,1)} %transpose_w.1.refs_4_.refs_3_), channel_id=1, source_target_pairs={{0,128},{128,256},{256,384},{384,0},{1,129},{129,257},{257,385},{3... | collective-permute-start | bytes 3145736 | tf_op jit(solution)/shard_map/ppermute | solution.py:27
  7.5 3.2 %collective-permute-start.4 = (bf16[512,1024]{1,0:T(8,128)(2,1)}, bf16[512,1024]{1,0:T(8,128)(2,1)S(1)}, u32[]{:S(2)}, u32[]{:S(2)}) collective-permute-start(bf16[512,1024]{1,0:T(8,128)(2,1)} %transpose_w.1.refs_4_.refs_3_), channel_id=1, source_target_pairs={{0,384},{128,0},{256,128},{384,256},{1,385},{129,1},{257,129},{385... | collective-permute-start | bytes 3145736 | tf_op jit(solution)/shard_map/ppermute | solution.py:27
  10.7 2.1 pack_kv.1
  12.8 11.7 %all-to-all-start = ((bf16[16,2,128,128]{3,2,1,0:T(8,128)(2,1)}), bf16[16,2,128,128]{3,2,1,0:T(8,128)(2,1)}, u32[]{:S(2)}, u32[]{:S(2)}) async-start(bf16[16,2,128,128]{3,2,1,0:T(8,128)(2,1)} %bitcast.11), calls=%async_computation | async-start | bytes 2097152 | tf_op jit(solution)/shard_map/all_to_all | solution.py:211
  24.6 1.4 collective-permute-done.3.refs_5_.refs_4_
  26.0 6.7 %collective-permute-start.5 = (bf16[256,1024]{1,0:T(8,128)(2,1)S(1)}, bf16[256,1024]{1,0:T(8,128)(2,1)S(1)}, u32[]{:S(2)}, u32[]{:S(2)}) collective-permute-start(bf16[256,1024]{1,0:T(8,128)(2,1)S(1)} %slice.16), channel_id=1, source_target_pairs={{0,128},{128,256},{256,384},{384,0},{1,129},{129,257},{257,385},{3... | collective-permute-start | bytes 1572872 | tf_op jit(solution)/shard_map/ppermute | solution.py:27
  32.9 4.2 %collective-permute-start.6 = (bf16[256,1024]{1,0:T(8,128)(2,1)S(1)}, bf16[256,1024]{1,0:T(8,128)(2,1)S(1)}, u32[]{:S(2)}, u32[]{:S(2)}) collective-permute-start(bf16[256,1024]{1,0:T(8,128)(2,1)S(1)} %slice.17), channel_id=1, source_target_pairs={{0,384},{128,0},{256,128},{384,256},{1,385},{129,1},{257,129},{385... | collective-permute-start | bytes 1572872 | tf_op jit(solution)/shard_map/ppermute | solution.py:27
  37.1 5.1 %collective-permute-start.7 = (bf16[512,1024]{1,0:T(8,128)(2,1)S(1)}, bf16[512,1024]{1,0:T(8,128)(2,1)}, u32[]{:S(2)}, u32[]{:S(2)}) collective-permute-start(bf16[512,1024]{1,0:T(8,128)(2,1)S(1)} %copy-done), channel_id=1, source_target_pairs={{0,1},{1,0},{2,3},{3,2},{4,5},{5,4},{6,7},{7,6},{8,9},{9,8},{10,11... | collective-permute-start | bytes 3145736 | tf_op jit(solution)/shard_map/ppermute | solution.py:27
  42.2 1.9 collective-permute-start.8
  44.1 2.4 %collective-permute-start.9 = (bf16[512,1024]{1,0:T(8,128)(2,1)S(1)}, bf16[512,1024]{1,0:T(8,128)(2,1)}, u32[]{:S(2)}, u32[]{:S(2)}) collective-permute-start(bf16[512,1024]{1,0:T(8,128)(2,1)S(1)} %collective-permute-done.4.refs_6_.refs_5_), channel_id=1, source_target_pairs={{0,1},{1,0},{2,3},{3,2},{4,5},{5,4},{6,7},{7,6},{8,9},{9,8},{10,11... | collective-permute-start | bytes 3145736 | tf_op jit(solution)/shard_map/ppermute | solution.py:27
  46.5 0.8 constant_dynamic-update-slice_fusion.1
  47.4 0.8 constant_dynamic-update-slice_fusion.refs_7_.refs_6_
  48.2 4.4 %collective-permute-start.10 = (bf16[512,1024]{1,0:T(8,128)(2,1)}, bf16[512,1024]{1,0:T(8,128)(2,1)}, u32[]{:S(2)}, u32[]{:S(2)}) collective-permute-start(bf16[512,1024]{1,0:T(8,128)(2,1)} %constant_dynamic-update-slice_fusion.refs_7_.refs_6_), channel_id=1, source_target_pairs={{0,1},{1,0},{2,3},{3,2},{4,5},{5,4},{6,7},{7,6},{8,9},{9,8},{10,11... | collective-permute-start | bytes 3145736 | tf_op jit(solution)/shard_map/ppermute | solution.py:27
  52.6 1.9 collective-permute-start
  55.8 0.7 copy-done.18
  57.1 1.9 pad_add_fusion.s_ref
  58.9 0.6 copy-done.14
  59.6 8.2 %attend.1.refs_1_ = bf16[2,64,1024]{2,1,0:T(8,128)(2,1)} custom-call(s32[4]{0:T(128)} %pad_add_fusion.s_ref, bf16[128,1024]{1,0:T(8,128)(2,1)} %mine_ref.1, bf16[64,1024]{1,0:T(8,128)(2,1)} %copy-done.14, bf16[16,2,128,128]{3,2,1,0:T(8,128)(2,1)} %all-to-all-done.kv_ref, bf16[128,1024]{1,0:T(8,128)(2,1)} %dk_ref.1, bf16[128,1024]{1,0:T(8,128)(2,1)} %dv_ref.1), custom_call_target="tpu_custom_call" | custom-call | tf_op jit(solution)/shard_map/attend/pallas_call | solution.py:96
  67.7 3.9 %collective-permute-start.1 = (bf16[2,64,1024]{2,1,0:T(8,128)(2,1)}, bf16[2,64,1024]{2,1,0:T(8,128)(2,1)S(1)}, u32[]{:S(2)}, u32[]{:S(2)}) collective-permute-start(bf16[2,64,1024]{2,1,0:T(8,128)(2,1)} %attend.1.refs_1_), channel_id=1, source_target_pairs={{0,16},{16,32},{32,48},{48,64},{64,80},{80,96},{96,112},{112,0},{1... | collective-permute-start | bytes 786440 | tf_op jit(solution)/shard_map/ppermute | solution.py:27
  71.7 3.8 %collective-permute-start.2 = (bf16[2,64,1024]{2,1,0:T(8,128)(2,1)}, bf16[2,64,1024]{2,1,0:T(8,128)(2,1)S(1)}, u32[]{:S(2)}, u32[]{:S(2)}) collective-permute-start(bf16[2,64,1024]{2,1,0:T(8,128)(2,1)} %attend.1.refs_1_), channel_id=1, source_target_pairs={{0,112},{16,0},{32,16},{48,32},{64,48},{80,64},{96,80},{112,96},{1... | collective-permute-start | bytes 786440 | tf_op jit(solution)/shard_map/ppermute | solution.py:27
  75.5 2.5 %collective-permute-start.11 = (bf16[2,64,1024]{2,1,0:T(8,128)(2,1)}, bf16[2,64,1024]{2,1,0:T(8,128)(2,1)S(1)}, u32[]{:S(2)}, u32[]{:S(2)}) collective-permute-start(bf16[2,64,1024]{2,1,0:T(8,128)(2,1)} %attend.1.refs_1_), channel_id=1, source_target_pairs={{0,32},{16,48},{32,64},{48,80},{64,96},{80,112},{96,0},{112,16},{1... | collective-permute-start | bytes 786440 | tf_op jit(solution)/shard_map/ppermute | solution.py:27
  78.0 4.9 %collective-permute-start.12 = (bf16[2,64,1024]{2,1,0:T(8,128)(2,1)}, bf16[2,64,1024]{2,1,0:T(8,128)(2,1)S(1)}, u32[]{:S(2)}, u32[]{:S(2)}) collective-permute-start(bf16[2,64,1024]{2,1,0:T(8,128)(2,1)} %attend.1.refs_1_), channel_id=1, source_target_pairs={{0,96},{16,112},{32,0},{48,16},{64,32},{80,48},{96,64},{112,80},{1... | collective-permute-start | bytes 786440 | tf_op jit(solution)/shard_map/ppermute | solution.py:27
  83.0 0.7 broadcast_in_dim.9.refs_12_
  83.8 7.0 %project.3 = (bf16[4,8,32,384]{3,2,1,0:T(8,128)(2,1)}, f32[8,128]{1,0:T(8,128)}) custom-call(s32[1]{0:T(128)} %bitcast.2.refs_0_, bf16[2,64,1024]{2,1,0:T(8,128)(2,1)} %attend.1.refs_1_, bf16[2,64,1024]{2,1,0:T(8,128)(2,1)} %copy-done.12, bf16[2,64,1024]{2,1,0:T(8,128)(2,1)} %copy-done.13, bf16[512,1024]{1,0:T(8,128)(2,1)} %transpose_w.1.refs_4_.refs_3_, ...), custom_call_target="tpu_custom_call" | custom-call | tf_op jit(solution)/shard_map/project/pallas_call | solution.py:134
  90.8 2.6 %collective-permute-done.11.refs_1_ = bf16[2,64,1024]{2,1,0:T(8,128)(2,1)S(1)} collective-permute-done((bf16[2,64,1024]{2,1,0:T(8,128)(2,1)}, bf16[2,64,1024]{2,1,0:T(8,128)(2,1)S(1)}, u32[]{:S(2)}, u32[]{:S(2)}) %collective-permute-start.11) | collective-permute-done | bytes 262176 | tf_op jit(solution)/shard_map/ppermute | solution.py:27
  93.4 3.5 %collective-permute-done.12.refs_2_ = bf16[2,64,1024]{2,1,0:T(8,128)(2,1)S(1)} collective-permute-done((bf16[2,64,1024]{2,1,0:T(8,128)(2,1)}, bf16[2,64,1024]{2,1,0:T(8,128)(2,1)S(1)}, u32[]{:S(2)}, u32[]{:S(2)}) %collective-permute-start.12) | collective-permute-done | bytes 262176 | tf_op jit(solution)/shard_map/ppermute | solution.py:27
  96.9 0.7 copy-done.8
  97.6 6.8 %project.4 = (bf16[4,8,32,256]{3,2,1,0:T(8,128)(2,1)}, f32[8,128]{1,0:T(8,128)}) custom-call(s32[1]{0:T(128)} %bitcast.2.refs_0_, bf16[2,64,1024]{2,1,0:T(8,128)(2,1)} %copy-done.6, bf16[2,64,1024]{2,1,0:T(8,128)(2,1)} %copy-done.8, bf16[512,1024]{1,0:T(8,128)(2,1)} %transpose_w.1.refs_4_.refs_3_, bf16[512,1024]{1,0:T(8,128)(2,1)} %copy-done.1, ...), custom_call_target="tpu_custom_call" | custom-call | tf_op jit(solution)/shard_map/project/pallas_call | solution.py:134
  104.4 27.8 %all_to_all.25 = bf16[32,32,256]{2,1,0:T(8,128)(2,1)} all-to-all(bf16[32,32,256]{2,1,0:T(8,128)(2,1)} %bitcast.16), channel_id=1, replica_groups=mesh['x'=4,'y'=8,'z'=8,'c'=2] {'x','z'}, dimensions={0} | all-to-all | bytes 1048576 | tf_op jit(solution)/shard_map/all_to_all | solution.py:211
  132.2 7.7 %all-to-all-start.1 = ((bf16[32,32,384]{2,1,0:T(8,128)(2,1)}), bf16[32,32,384]{2,1,0:T(8,128)(2,1)S(1)}, u32[]{:S(2)}, u32[]{:S(2)}) async-start(bf16[32,32,384]{2,1,0:T(8,128)(2,1)} %bitcast.5), calls=%async_computation.1 | async-start | bytes 1572864 | tf_op jit(solution)/shard_map/all_to_all | solution.py:211
  139.9 1.9 collective-permute-start.13
  141.9 4.6 %collective-permute-start.14 = (bf16[2,64,1024]{2,1,0:T(8,128)(2,1)S(1)}, bf16[2,64,1024]{2,1,0:T(8,128)(2,1)S(1)}, u32[]{:S(2)}, u32[]{:S(2)}) collective-permute-start(bf16[2,64,1024]{2,1,0:T(8,128)(2,1)S(1)} %copy-done.9), channel_id=1, source_target_pairs={{0,112},{16,0},{32,16},{48,32},{64,48},{80,64},{96,80},{112,96},{1... | collective-permute-start | bytes 786440 | tf_op jit(solution)/shard_map/ppermute | solution.py:27
  146.5 2.1 collective-permute-start.16
  148.6 4.1 %collective-permute-start.15 = (bf16[1,64,1024]{2,1,0:T(8,128)(2,1)S(1)}, bf16[1,64,1024]{2,1,0:T(8,128)(2,1)S(1)}, u32[]{:S(2)}, u32[]{:S(2)}) collective-permute-start(bf16[1,64,1024]{2,1,0:T(8,128)(2,1)S(1)} %slice.18), channel_id=1, source_target_pairs={{0,32},{16,48},{32,64},{48,80},{64,96},{80,112},{96,0},{112,16},{1... | collective-permute-start | bytes 393224 | tf_op jit(solution)/shard_map/ppermute | solution.py:27
  152.7 4.5 %collective-permute-done.16 = bf16[1,64,1024]{2,1,0:T(8,128)(2,1)S(1)} collective-permute-done((bf16[1,64,1024]{2,1,0:T(8,128)(2,1)S(1)}, bf16[1,64,1024]{2,1,0:T(8,128)(2,1)S(1)}, u32[]{:S(2)}, u32[]{:S(2)}) %collective-permute-start.16) | collective-permute-done | bytes 131104 | tf_op jit(solution)/shard_map/ppermute | solution.py:27
  157.2 1.6 collective-permute-done.15
  158.7 0.7 pad_maximum_fusion.refs_3_
  159.5 0.7 copy-done.10
  160.2 7.0 %project.5 = (bf16[4,8,32,384]{3,2,1,0:T(8,128)(2,1)}, f32[8,128]{1,0:T(8,128)}) custom-call(s32[1]{0:T(128)} %bitcast.2.refs_0_, bf16[2,64,1024]{2,1,0:T(8,128)(2,1)} %copy-done.10, bf16[2,64,1024]{2,1,0:T(8,128)(2,1)} %copy-done.11, bf16[2,64,1024]{2,1,0:T(8,128)(2,1)} %pad_maximum_fusion.refs_3_, bf16[512,1024]{1,0:T(8,128)(2,1)} %transpose_w.1.refs_4_.refs_3_, ...), custom_call_target="tpu_custom_call" | custom-call | tf_op jit(solution)/shard_map/project/pallas_call | solution.py:134
  167.3 0.9 copy-done.3
  168.2 7.8 %all-to-all-start.3 = ((bf16[32,32,384]{2,1,0:T(8,128)(2,1)}), bf16[32,32,384]{2,1,0:T(8,128)(2,1)S(1)}, u32[]{:S(2)}, u32[]{:S(2)}) async-start(bf16[32,32,384]{2,1,0:T(8,128)(2,1)} %bitcast.15), calls=%async_computation.3 | async-start | bytes 1572864 | tf_op jit(solution)/shard_map/all_to_all | solution.py:211
  176.7 0.6 concatenate.12.s_ref
  177.3 14.9 %all-to-all-done.3 = bf16[32,32,384]{2,1,0:T(8,128)(2,1)S(1)} async-done(((bf16[32,32,384]{2,1,0:T(8,128)(2,1)}), bf16[32,32,384]{2,1,0:T(8,128)(2,1)S(1)}, u32[]{:S(2)}, u32[]{:S(2)}) %all-to-all-start.3) | async-done | bytes 786464 | tf_op jit(solution)/shard_map/all_to_all | solution.py:211
  192.2 0.9 copy-done.4
  193.1 2.9 %place.1 = bf16[16,32,384]{2,1,0:T(8,128)(2,1)} custom-call(s32[194]{0:T(256)} %concatenate.12.s_ref, bf16[4,8,32,384]{3,2,1,0:T(8,128)(2,1)} %bitcast.12, bf16[4,8,32,256]{3,2,1,0:T(8,128)(2,1)} %bitcast.14, bf16[4,8,32,384]{3,2,1,0:T(8,128)(2,1)} %bitcast.13), custom_call_target="tpu_custom_call" | custom-call | tf_op jit(solution)/shard_map/place/pallas_call | solution.py:175
  196.1 26.3 %all_to_all.26.i_ref = bf16[16,32,384]{2,1,0:T(8,128)(2,1)} all-to-all(bf16[16,32,384]{2,1,0:T(8,128)(2,1)} %place.1), channel_id=1, replica_groups=mesh['x'=4,'y'=8,'z'=8,'c'=2] {'z','c'}, dimensions={0} | all-to-all | bytes 786432 | tf_op jit(solution)/shard_map/all_to_all | solution.py:211
  222.3 1.9 finish.1
  (53 shorter events, 2.9 us)
Async XLA Ops:
  3.6 22.4 %collective-permute-start.3 = (bf16[512,1024]{1,0:T(8,128)(2,1)}, bf16[512,1024]{1,0:T(8,128)(2,1)S(1)}, u32[]{:S(2)}, u32[]{:S(2)}) collective-permute-start(bf16[512,1024]{1,0:T(8,128)(2,1)} %transpose_w.1.refs_4_.refs_3_), channel_id=1, source_target_pairs={{0,128},{128,256},{256,384},{384,0},{1,129},{129,257},{257,385},{3... | collective-permute-start | bytes 3145736 | tf_op jit(solution)/shard_map/ppermute | solution.py:27
  7.5 25.3 %collective-permute-start.4 = (bf16[512,1024]{1,0:T(8,128)(2,1)}, bf16[512,1024]{1,0:T(8,128)(2,1)S(1)}, u32[]{:S(2)}, u32[]{:S(2)}) collective-permute-start(bf16[512,1024]{1,0:T(8,128)(2,1)} %transpose_w.1.refs_4_.refs_3_), channel_id=1, source_target_pairs={{0,384},{128,0},{256,128},{384,256},{1,385},{129,1},{257,129},{385... | collective-permute-start | bytes 3145736 | tf_op jit(solution)/shard_map/ppermute | solution.py:27
  12.8 46.1 %all-to-all-start = ((bf16[16,2,128,128]{3,2,1,0:T(8,128)(2,1)}), bf16[16,2,128,128]{3,2,1,0:T(8,128)(2,1)}, u32[]{:S(2)}, u32[]{:S(2)}) async-start(bf16[16,2,128,128]{3,2,1,0:T(8,128)(2,1)} %bitcast.11), calls=%async_computation | async-start | bytes 2097152 | tf_op jit(solution)/shard_map/all_to_all | solution.py:211
  24.6 12.5 %copy-start = (bf16[512,1024]{1,0:T(8,128)(2,1)S(1)}, bf16[512,1024]{1,0:T(8,128)(2,1)}, u32[]{:S(2)}) copy-start(bf16[512,1024]{1,0:T(8,128)(2,1)} %transpose_w.1.refs_4_.refs_3_) | copy-start | bytes 3145732
  26.0 16.2 %copy-start.1 = (bf16[512,1024]{1,0:T(8,128)(2,1)}, bf16[512,1024]{1,0:T(8,128)(2,1)S(1)}, u32[]{:S(2)}) copy-start(bf16[512,1024]{1,0:T(8,128)(2,1)S(1)} %collective-permute-done.3.refs_5_.refs_4_) | copy-start | bytes 3145732
  26.0 20.5 %collective-permute-start.5 = (bf16[256,1024]{1,0:T(8,128)(2,1)S(1)}, bf16[256,1024]{1,0:T(8,128)(2,1)S(1)}, u32[]{:S(2)}, u32[]{:S(2)}) collective-permute-start(bf16[256,1024]{1,0:T(8,128)(2,1)S(1)} %slice.16), channel_id=1, source_target_pairs={{0,128},{128,256},{256,384},{384,0},{1,129},{129,257},{257,385},{3... | collective-permute-start | bytes 1572872 | tf_op jit(solution)/shard_map/ppermute | solution.py:27
  32.8 14.6 %copy-start.2 = (bf16[512,1024]{1,0:T(8,128)(2,1)}, bf16[512,1024]{1,0:T(8,128)(2,1)S(1)}, u32[]{:S(2)}) copy-start(bf16[512,1024]{1,0:T(8,128)(2,1)S(1)} %collective-permute-done.4.refs_6_.refs_5_) | copy-start | bytes 3145732
  32.9 14.5 %collective-permute-start.6 = (bf16[256,1024]{1,0:T(8,128)(2,1)S(1)}, bf16[256,1024]{1,0:T(8,128)(2,1)S(1)}, u32[]{:S(2)}, u32[]{:S(2)}) collective-permute-start(bf16[256,1024]{1,0:T(8,128)(2,1)S(1)} %slice.17), channel_id=1, source_target_pairs={{0,384},{128,0},{256,128},{384,256},{1,385},{129,1},{257,129},{385... | collective-permute-start | bytes 1572872 | tf_op jit(solution)/shard_map/ppermute | solution.py:27
  37.1 34.6 %collective-permute-start.7 = (bf16[512,1024]{1,0:T(8,128)(2,1)S(1)}, bf16[512,1024]{1,0:T(8,128)(2,1)}, u32[]{:S(2)}, u32[]{:S(2)}) collective-permute-start(bf16[512,1024]{1,0:T(8,128)(2,1)S(1)} %copy-done), channel_id=1, source_target_pairs={{0,1},{1,0},{2,3},{3,2},{4,5},{5,4},{6,7},{7,6},{8,9},{9,8},{10,11... | collective-permute-start | bytes 3145736 | tf_op jit(solution)/shard_map/ppermute | solution.py:27
  42.2 33.3 %collective-permute-start.8 = (bf16[512,1024]{1,0:T(8,128)(2,1)S(1)}, bf16[512,1024]{1,0:T(8,128)(2,1)}, u32[]{:S(2)}, u32[]{:S(2)}) collective-permute-start(bf16[512,1024]{1,0:T(8,128)(2,1)S(1)} %collective-permute-done.3.refs_5_.refs_4_), channel_id=1, source_target_pairs={{0,1},{1,0},{2,3},{3,2},{4,5},{5,4},{6,7},{7,6},{8,9},{9,8},{10,11... | collective-permute-start | bytes 3145736 | tf_op jit(solution)/shard_map/ppermute | solution.py:27
  44.1 33.9 %collective-permute-start.9 = (bf16[512,1024]{1,0:T(8,128)(2,1)S(1)}, bf16[512,1024]{1,0:T(8,128)(2,1)}, u32[]{:S(2)}, u32[]{:S(2)}) collective-permute-start(bf16[512,1024]{1,0:T(8,128)(2,1)S(1)} %collective-permute-done.4.refs_6_.refs_5_), channel_id=1, source_target_pairs={{0,1},{1,0},{2,3},{3,2},{4,5},{5,4},{6,7},{7,6},{8,9},{9,8},{10,11... | collective-permute-start | bytes 3145736 | tf_op jit(solution)/shard_map/ppermute | solution.py:27
  47.4 5.2 %copy-start.5 = (bf16[128,1024]{1,0:T(8,128)(2,1)S(1)}, bf16[128,1024]{1,0:T(8,128)(2,1)}, u32[]{:S(2)}) copy-start(bf16[128,1024]{1,0:T(8,128)(2,1)} %mine_ref.1) | copy-start | bytes 786436
  48.2 34.7 %collective-permute-start.10 = (bf16[512,1024]{1,0:T(8,128)(2,1)}, bf16[512,1024]{1,0:T(8,128)(2,1)}, u32[]{:S(2)}, u32[]{:S(2)}) collective-permute-start(bf16[512,1024]{1,0:T(8,128)(2,1)} %constant_dynamic-update-slice_fusion.refs_7_.refs_6_), channel_id=1, source_target_pairs={{0,1},{1,0},{2,3},{3,2},{4,5},{5,4},{6,7},{7,6},{8,9},{9,8},{10,11... | collective-permute-start | bytes 3145736 | tf_op jit(solution)/shard_map/ppermute | solution.py:27
  52.6 6.3 %collective-permute-start = (bf16[64,1024]{1,0:T(8,128)(2,1)S(1)}, bf16[64,1024]{1,0:T(8,128)(2,1)S(1)}, u32[]{:S(2)}, u32[]{:S(2)}) collective-permute-start(bf16[64,1024]{1,0:T(8,128)(2,1)S(1)} %constant_dynamic-slice_fusion), channel_id=1, source_target_pairs={{0,1},{1,0},{2,3},{3,2},{4,5},{5,4},{6,7},{7,6},{8,9},{9,8},{10,11... | collective-permute-start | bytes 393224 | tf_op jit(solution)/shard_map/ppermute | solution.py:27
  54.6 0.7 copy-start.15
  55.8 0.7 copy-start.18
  58.9 0.7 copy-start.14
  67.7 15.2 %collective-permute-start.1 = (bf16[2,64,1024]{2,1,0:T(8,128)(2,1)}, bf16[2,64,1024]{2,1,0:T(8,128)(2,1)S(1)}, u32[]{:S(2)}, u32[]{:S(2)}) collective-permute-start(bf16[2,64,1024]{2,1,0:T(8,128)(2,1)} %attend.1.refs_1_), channel_id=1, source_target_pairs={{0,16},{16,32},{32,48},{48,64},{64,80},{80,96},{96,112},{112,0},{1... | collective-permute-start | bytes 786440 | tf_op jit(solution)/shard_map/ppermute | solution.py:27
  71.7 11.3 %collective-permute-start.2 = (bf16[2,64,1024]{2,1,0:T(8,128)(2,1)}, bf16[2,64,1024]{2,1,0:T(8,128)(2,1)S(1)}, u32[]{:S(2)}, u32[]{:S(2)}) collective-permute-start(bf16[2,64,1024]{2,1,0:T(8,128)(2,1)} %attend.1.refs_1_), channel_id=1, source_target_pairs={{0,112},{16,0},{32,16},{48,32},{64,48},{80,64},{96,80},{112,96},{1... | collective-permute-start | bytes 786440 | tf_op jit(solution)/shard_map/ppermute | solution.py:27
  75.5 17.9 %collective-permute-start.11 = (bf16[2,64,1024]{2,1,0:T(8,128)(2,1)}, bf16[2,64,1024]{2,1,0:T(8,128)(2,1)S(1)}, u32[]{:S(2)}, u32[]{:S(2)}) collective-permute-start(bf16[2,64,1024]{2,1,0:T(8,128)(2,1)} %attend.1.refs_1_), channel_id=1, source_target_pairs={{0,32},{16,48},{32,64},{48,80},{64,96},{80,112},{96,0},{112,16},{1... | collective-permute-start | bytes 786440 | tf_op jit(solution)/shard_map/ppermute | solution.py:27
  78.0 18.9 %collective-permute-start.12 = (bf16[2,64,1024]{2,1,0:T(8,128)(2,1)}, bf16[2,64,1024]{2,1,0:T(8,128)(2,1)S(1)}, u32[]{:S(2)}, u32[]{:S(2)}) collective-permute-start(bf16[2,64,1024]{2,1,0:T(8,128)(2,1)} %attend.1.refs_1_), channel_id=1, source_target_pairs={{0,96},{16,112},{32,0},{48,16},{64,32},{80,48},{96,64},{112,80},{1... | collective-permute-start | bytes 786440 | tf_op jit(solution)/shard_map/ppermute | solution.py:27
  82.9 0.7 copy-start.12
  82.9 0.8 copy-start.13
  93.4 3.5 %copy-start.6 = (bf16[2,64,1024]{2,1,0:T(8,128)(2,1)}, bf16[2,64,1024]{2,1,0:T(8,128)(2,1)S(1)}, u32[]{:S(2)}) copy-start(bf16[2,64,1024]{2,1,0:T(8,128)(2,1)S(1)} %collective-permute-done.11.refs_1_) | copy-start | bytes 786436
  96.9 0.7 copy-start.8
  132.2 7.8 %copy-start.7 = (bf16[2,64,1024]{2,1,0:T(8,128)(2,1)S(1)}, bf16[2,64,1024]{2,1,0:T(8,128)(2,1)}, u32[]{:S(2)}) copy-start(bf16[2,64,1024]{2,1,0:T(8,128)(2,1)} %copy-done.6) | copy-start | bytes 786436
  132.2 9.7 %copy-start.9 = (bf16[2,64,1024]{2,1,0:T(8,128)(2,1)S(1)}, bf16[2,64,1024]{2,1,0:T(8,128)(2,1)}, u32[]{:S(2)}) copy-start(bf16[2,64,1024]{2,1,0:T(8,128)(2,1)} %copy-done.8) | copy-start | bytes 786436
  132.2 35.1 %all-to-all-start.1 = ((bf16[32,32,384]{2,1,0:T(8,128)(2,1)}), bf16[32,32,384]{2,1,0:T(8,128)(2,1)S(1)}, u32[]{:S(2)}, u32[]{:S(2)}) async-start(bf16[32,32,384]{2,1,0:T(8,128)(2,1)} %bitcast.5), calls=%async_computation.1 | async-start | bytes 1572864 | tf_op jit(solution)/shard_map/all_to_all | solution.py:211
  139.9 19.5 %collective-permute-start.13 = (bf16[2,64,1024]{2,1,0:T(8,128)(2,1)S(1)}, bf16[2,64,1024]{2,1,0:T(8,128)(2,1)S(1)}, u32[]{:S(2)}, u32[]{:S(2)}) collective-permute-start(bf16[2,64,1024]{2,1,0:T(8,128)(2,1)S(1)} %copy-done.7), channel_id=1, source_target_pairs={{0,16},{16,32},{32,48},{48,64},{64,80},{80,96},{96,112},{112,0},{1... | collective-permute-start | bytes 786440 | tf_op jit(solution)/shard_map/ppermute | solution.py:27
  141.9 17.6 %collective-permute-start.14 = (bf16[2,64,1024]{2,1,0:T(8,128)(2,1)S(1)}, bf16[2,64,1024]{2,1,0:T(8,128)(2,1)S(1)}, u32[]{:S(2)}, u32[]{:S(2)}) collective-permute-start(bf16[2,64,1024]{2,1,0:T(8,128)(2,1)S(1)} %copy-done.9), channel_id=1, source_target_pairs={{0,112},{16,0},{32,16},{48,32},{64,48},{80,64},{96,80},{112,96},{1... | collective-permute-start | bytes 786440 | tf_op jit(solution)/shard_map/ppermute | solution.py:27
  146.5 10.7 %collective-permute-start.16 = (bf16[1,64,1024]{2,1,0:T(8,128)(2,1)S(1)}, bf16[1,64,1024]{2,1,0:T(8,128)(2,1)S(1)}, u32[]{:S(2)}, u32[]{:S(2)}) collective-permute-start(bf16[1,64,1024]{2,1,0:T(8,128)(2,1)S(1)} %slice.19), channel_id=1, source_target_pairs={{0,96},{16,112},{32,0},{48,16},{64,32},{80,48},{96,64},{112,80},{1... | collective-permute-start | bytes 393224 | tf_op jit(solution)/shard_map/ppermute | solution.py:27
  148.6 10.1 %collective-permute-start.15 = (bf16[1,64,1024]{2,1,0:T(8,128)(2,1)S(1)}, bf16[1,64,1024]{2,1,0:T(8,128)(2,1)S(1)}, u32[]{:S(2)}, u32[]{:S(2)}) collective-permute-start(bf16[1,64,1024]{2,1,0:T(8,128)(2,1)S(1)} %slice.18), channel_id=1, source_target_pairs={{0,32},{16,48},{32,64},{48,80},{64,96},{80,112},{96,0},{112,16},{1... | collective-permute-start | bytes 393224 | tf_op jit(solution)/shard_map/ppermute | solution.py:27
  159.5 0.7 copy-start.10
  159.5 0.8 copy-start.11
  167.3 0.9 copy-start.3
  168.2 24.0 %all-to-all-start.3 = ((bf16[32,32,384]{2,1,0:T(8,128)(2,1)}), bf16[32,32,384]{2,1,0:T(8,128)(2,1)S(1)}, u32[]{:S(2)}, u32[]{:S(2)}) async-start(bf16[32,32,384]{2,1,0:T(8,128)(2,1)} %bitcast.15), calls=%async_computation.3 | async-start | bytes 1572864 | tf_op jit(solution)/shard_map/all_to_all | solution.py:211
  176.0 0.7 copy-start.16
  176.0 0.7 copy-start.17
  192.2 0.9 copy-start.4
where the time goes:
time: 225 us; the launch traced here: 224 us
  starting transfers between devices  88.8 us (39%)
  blocking collectives  54.1 us (24%)
  Pallas kernels  39.5 us (18%)
  waiting for transfers between devices  28.5 us (13%)
  local copies, waits for them, and re-layouts  10.4 us (5%)
  other arithmetic  2.57 us (1%)
    ppermute x17, starting transfers between devices, shift(): lax.ppermute(value, axis, [(i, (i + step) % size) for i in range(size)])  61.5 us
    all_to_all x2, blocking collectives, exchange(): return lax.all_to_all(value, axes, 0, 0, tiled=True)  54.1 us
    all_to_all x3, starting transfers between devices, exchange(): return lax.all_to_all(value, axes, 0, 0, tiled=True)  27.3 us
    pallas_call x3, Pallas kernels, project(): pl.pallas_call(lambda *refs: project_kernel(count, *refs), in_specs=[SMEM...  20.8 us
    all_to_all x3, waiting for transfers between devices, exchange(): return lax.all_to_all(value, axes, 0, 0, tiled=True)  14.9 us
    ppermute x17, waiting for transfers between devices, shift(): lax.ppermute(value, axis, [(i, (i + step) % size) for i in range(size)])  13.6 us
    pallas_call x1, Pallas kernels, attend(): pl.pallas_call(attend_kernel, grid_spec=pltpu.PrefetchScalarGridSpec(num_...  8.15 us
    unnamed x39, local copies, waits for them, and re-layouts  6.89 us
  transfers between devices with their start and end apart: 20, of which 6 were waited for; matrix products, arithmetic and copies ran while one was open for 3% of the time, Pallas kernels for 11%

commit v1 on v0

--- a/solution.py
+++ b/solution.py
@@ -9,7 +9,6 @@
 HEAD_DIM = 128
 DRAFT = 64
 PACK = 96
-REQUESTS = 64
 NX, NY, NZ = 4, 8, 8
 NEG_FILL = -1e30
 BF16 = jnp.bfloat16
@@ -20,11 +19,16 @@
 ANY = pl.BlockSpec(memory_space=pl.ANY)
 TOKEN = jax.ShapeDtypeStruct((8, 128), F32)
 
-CHUNKS = ((0, -1, 1), (-2, 2), (-3, 3, -4))
+CHUNKS = ((0, -1, 1, -2), (2, -3, 3, -4))
 
 
 def shift(value, axis, size, step):
     return lax.ppermute(value, axis, [(i, (i + step) % size) for i in range(size)])
+
+
+def shift_cores(value, axis, size, step):
+    pairs = [(2 * i + c, 2 * ((i + step * (1 - 2 * c)) % size) + c) for i in range(size) for c in (0, 1)]
+    return lax.ppermute(value, (axis, "c"), pairs)
 
 
 def kv_kernel(k_ref, v_ref, o_ref):
@@ -59,9 +63,9 @@
     )(w)
 
 
-def attend_kernel(s_ref, mine_ref, other_ref, kv_ref, dk_ref, dv_ref, o_ref):
-    cache_len = s_ref[2]
-    draft_len = s_ref[3]
+def attend_kernel(s_ref, cache_ref, draft_ref, mine_ref, other_ref, kv_ref, dk_ref, dv_ref, o_ref):
+    cache_len = cache_ref[s_ref[3]]
+    draft_len = draft_ref[(s_ref[0] * NY + s_ref[1]) * 2 + s_ref[3]]
     scale = HEAD_DIM ** (-0.5)
     keys = kv_ref[:, 0].reshape(2048, HEAD_DIM)
     values = kv_ref[:, 1].reshape(2048, HEAD_DIM)
@@ -91,60 +95,67 @@
         o_ref[side, :, HEAD_DIM:] = mixed[DRAFT:]
 
 
-def attend(scalars, q, other_q, kv, dk, dv):
-    draft = pl.BlockSpec((DRAFT, HEAD_DIM), lambda p, s: (s[1], s[0]))
+def attend(ids, cache_lengths, draft_lengths, q, other_q, kv, dk, dv):
+    draft = pl.BlockSpec((DRAFT, HEAD_DIM), lambda p, s, *_: (s[3], s[2]))
     return pl.pallas_call(
         attend_kernel,
         grid_spec=pltpu.PrefetchScalarGridSpec(
-            num_scalar_prefetch=1,
+            num_scalar_prefetch=3,
             grid=(4,),
             in_specs=[
-                pl.BlockSpec((DRAFT, 256), lambda p, s: (s[1], p)),
-                pl.BlockSpec((DRAFT, 256), lambda p, s: (0, p)),
-                pl.BlockSpec((16, 2, 128, 128), lambda p, s: (0, 0, 0, 0)),
+                pl.BlockSpec((DRAFT, 256), lambda p, s, *_: (s[3], p)),
+                pl.BlockSpec((DRAFT, 256), lambda p, *_: (0, p)),
+                pl.BlockSpec((16, 2, 128, 128), lambda p, *_: (0, 0, 0, 0)),
                 draft,
                 draft,
             ],
-            out_specs=pl.BlockSpec((2, DRAFT, 256), lambda p, s: (0, 0, p)),
+            out_specs=pl.BlockSpec((2, DRAFT, 256), lambda p, *_: (0, 0, p)),
         ),
         out_shape=jax.ShapeDtypeStruct((2, DRAFT, 1024), BF16),
         name="attend",
-    )(scalars, q, other_q, kv, dk, dv)
+    )(ids, cache_lengths, draft_lengths, q, other_q, kv, dk, dv)
 
 
 def project_kernel(count, s_ref, *refs):
-    rows, own, far = refs[:count], refs[count : count + 4], refs[count + 4 : count + 8]
-    o_ref, token_ref = refs[-2:]
+    rows, weights = refs[:count], refs[count : count + 8]
+    o_ref, token_ref, w_ref, sems = refs[-4:]
+    copies = [pltpu.make_async_copy(w, w_ref.at[i], sems.at[i]) for i, w in enumerate(weights)]
+    for copy in copies[:4]:
+        copy.start()
     token_ref[...] = jnp.zeros(token_ref.shape, F32)
-    x = s_ref[0]
     width = count * DRAFT
     a = jnp.concatenate([ref[0] for ref in rows], axis=0)
     b = jnp.concatenate([ref[1] for ref in rows], axis=0)
-    for step, own_ref, far_ref in zip((0, -1, 1, 2), own, far):
-        acc = lax.dot_general(own_ref[...], a, NT, preferred_element_type=F32)
-        acc = acc + lax.dot_general(far_ref[...], b, NT, preferred_element_type=F32)
+    for i, step in enumerate((0, -1, 1, 2)):
+        if i > 0 and 2 * i + 2 < 8:
+            copies[2 * i + 2].start()
+            copies[2 * i + 3].start()
+        copies[2 * i].wait()
+        copies[2 * i + 1].wait()
+        acc = lax.dot_general(w_ref[2 * i], a, NT, preferred_element_type=F32)
+        acc = acc + lax.dot_general(w_ref[2 * i + 1], b, NT, preferred_element_type=F32)
         acc = acc.astype(BF16).reshape(NZ, 2, 32, width)
-        at = lax.rem(x + step + NX, NX)
+        at = lax.rem(s_ref[0] + step + NX, NX)
         for half in range(2):
             o_ref[at, :, :, half * width : (half + 1) * width] = acc[:, half]
 
 
-def project(x, rows, own, far, token):
+def project(ids, rows, weights, token):
     count = len(rows)
     return pl.pallas_call(
         lambda *refs: project_kernel(count, *refs),
-        in_specs=[SMEM] + [VMEM] * (count + 8) + [ANY],
+        in_specs=[SMEM] + [VMEM] * count + [pl.BlockSpec(memory_space=pltpu.HBM)] * 8 + [ANY],
         out_specs=[VMEM, VMEM],
         out_shape=[jax.ShapeDtypeStruct((NX, NZ, 32, 2 * count * DRAFT), BF16), TOKEN],
+        scratch_shapes=[pltpu.VMEM((8, 512, 1024), BF16), pltpu.SemaphoreType.DMA((8,))],
         name="project",
-    )(x, *rows, *own, *far, token)
-
-
-def place_kernel(s_ref, *refs):
+    )(ids, *rows, *weights, token)
+
+
+def place_kernel(s_ref, length_ref, group_ref, first_ref, *refs):
     parts, o_ref, f_ref = refs[:-2], refs[-2], refs[-1]
     f_ref[...] = jnp.zeros(f_ref.shape, F32)
-    my_y = s_ref[3 * REQUESTS]
-    core = s_ref[3 * REQUESTS + 1]
+    my_y, core = s_ref[1], s_ref[3]
     lane = lax.broadcasted_iota(jnp.int32, (32, 128), 1)
     for x in range(NX):
         for slots, ref in zip(CHUNKS, parts):
@@ -156,9 +167,7 @@
                 for part in range(2):
                     column, at = divmod(2 * tile + part, len(slots))
                     request = (x * NY + lax.rem(my_y + slots[at] + NY, NY)) * 2 + core
-                    length = s_ref[request]
-                    group = s_ref[REQUESTS + request]
-                    first = s_ref[2 * REQUESTS + request]
+                    length, group, first = length_ref[request], group_ref[request], first_ref[request]
                     moved = pltpu.roll(slab, lax.rem(first + 64 * part, 128), 1)
                     keep = (lane >= first) & (lane < first + length)
                     spot = 2 * group + column
@@ -171,15 +180,15 @@
         o_ref[t, :, 256:] = jnp.where(lane < 32, c, d).astype(BF16)
 
 
-def place(scalars, parts):
+def place(tables, parts):
     return pl.pallas_call(
         place_kernel,
-        in_specs=[SMEM] + [VMEM] * len(parts),
+        in_specs=[SMEM] * len(tables) + [VMEM] * len(parts),
         out_specs=VMEM,
         out_shape=jax.ShapeDtypeStruct((16, 32, 4 * PACK), BF16),
         scratch_shapes=[pltpu.VMEM((64, 32, 128), F32)],
         name="place",
-    )(scalars, *parts)
+    )(*tables, *parts)
 
 
 def finish_kernel(i_ref, o_ref):
@@ -223,38 +232,35 @@
     dest_group,
     dest_offset,
 ):
-    x, y, z, c = (lax.axis_index(name).astype(jnp.int32) for name in ("x", "y", "z", "c"))
-    request = (x * NY + y) * 2 + c
-    cache_length = lax.dynamic_slice_in_dim(cache_lengths, c, 1)
-    draft_length = lax.dynamic_slice_in_dim(draft_lengths, request, 1)
-    scalars = jnp.concatenate([jnp.stack([z, c]), cache_length, draft_length])
-    table = jnp.concatenate([draft_lengths, dest_group, dest_offset, jnp.stack([y, c])])
+    c = lax.axis_index("c")
+    ids = jnp.stack([lax.axis_index(name) for name in ("x", "y", "z", "c")]).astype(jnp.int32)
 
     kv = exchange(pack_kv(cache_keys, cache_values).reshape(16, 2, 128, 128), ("z", "c"))
 
     w0 = transpose(out_weight)
     w1, w2 = shift(w0, "x", NX, 1), shift(w0, "x", NX, -1)
-    w3 = jnp.concatenate([shift(w1[:256], "x", NX, 1), shift(w2[256:], "x", NX, -1)], axis=0)
-    own = [w0, w1, w2, w3]
-    far = [shift(w, "c", 2, 1) for w in own]
+    w3 = shift_cores(jnp.where(c == 0, w1, w2), "x", NX, 1)
+    weights = []
+    for w in (w0, w1, w2, w3):
+        weights += [w, shift(w, "c", 2, 1)]
     other_q = lax.dynamic_slice_in_dim(queries, (1 - c) * DRAFT, DRAFT, 0)
     other_q = shift(other_q, "c", 2, 1)
 
-    rows = attend(scalars, queries, other_q, kv, draft_keys, draft_values)
+    rows = attend(ids, cache_lengths, draft_lengths, queries, other_q, kv, draft_keys, draft_values)
     up1, down1 = shift(rows, "y", NY, 1), shift(rows, "y", NY, -1)
     up2, down2 = shift(rows, "y", NY, 2), shift(rows, "y", NY, -2)
     up3, down3 = shift(up2, "y", NY, 1), shift(down2, "y", NY, -1)
-    up4, down4 = shift(up2[:1], "y", NY, 2), shift(down2[1:], "y", NY, -2)
-    arrived = {0: rows, -1: up1, 1: down1, -2: up2, 2: down2, -3: up3, 3: down3}
-    arrived[-4] = jnp.concatenate([up4, down4], axis=0)
+    far = shift_cores(jnp.where(c == 0, up2, down2), "y", NY, 2)
+    arrived = {0: rows, -1: up1, 1: down1, -2: up2, 2: down2, -3: up3, 3: down3, -4: far}
 
     token = jnp.zeros(TOKEN.shape, F32)
     sums = []
     for slots in CHUNKS:
-        part, token = project(x[None], [arrived[s] for s in slots], own, far, token)
+        part, token = project(ids, [arrived[s] for s in slots], weights, token)
         part = part.reshape(NX * NZ, 32, -1)
         sums.append(exchange(part, ("x", "z")).reshape(NX, NZ, 32, -1))
-    return finish(exchange(place(table, sums), ("z", "c")))
+    placed = place([ids, draft_lengths, dest_group, dest_offset], sums)
+    return finish(exchange(placed, ("z", "c")))
 
 
 def solution(mesh):

time: 225 us -> 214 us (0.951)
  the two profiles are of different devices: /device:TPU:1 before, /device:TPU:9 now
where the time goes in v1:
time: 214 us; the launch traced here: 213 us
  starting transfers between devices  84.5 us (39%)
  blocking collectives  57.3 us (27%)
  Pallas kernels  36.9 us (17%)
  waiting for transfers between devices  31.1 us (15%)
    all_to_all x2, blocking collectives, exchange(): return lax.all_to_all(value, axes, 0, 0, tiled=True)  57.3 us
    ppermute x13, starting transfers between devices, shift(): lax.ppermute(value, axis, [(i, (i + step) % size) for i in range(size)])  52.4 us
    all_to_all x2, starting transfers between devices, exchange(): return lax.all_to_all(value, axes, 0, 0, tiled=True)  23.3 us
    ppermute x13, waiting for transfers between devices, shift(): lax.ppermute(value, axis, [(i, (i + step) % size) for i in range(size)])  18.6 us
    pallas_call x2, Pallas kernels, project(): pl.pallas_call(lambda *refs: project_kernel(count, *refs), in_specs=[SMEM...  18.2 us
    ppermute x2, waiting for transfers between devices, shift_cores(): return lax.ppermute(value, (axis, 'c'), pairs)  12.5 us
    ppermute x2, starting transfers between devices, shift_cores(): return lax.ppermute(value, (axis, 'c'), pairs)  8.74 us
    pallas_call x1, Pallas kernels, attend(): pl.pallas_call(attend_kernel, grid_spec=pltpu.PrefetchScalarGridSpec(num_...  8.17 us
  transfers between devices with their start and end apart: 17, of which 8 were waited for; matrix products, arithmetic and copies ran while one was open for 0% of the time, Pallas kernels for 9%

profile of v1, /device:TPU:9, one launch (start us, length us, event | category | flops | bytes accessed | tf_op | source)
XLA Modules:
  0.0 213.1 jit_solution(14186946409607686028)
XLA Ops:
  0.0 3.6 %transpose_w.1.refs_5_ = bf16[512,1024]{1,0:T(8,128)(2,1)} custom-call(bf16[1024,512]{1,0:T(8,128)(2,1)} %w_ref.1), custom_call_target="tpu_custom_call" | custom-call | tf_op jit(solution)/shard_map/transpose_w/pallas_call | solution.py:56
  3.6 3.1 %collective-permute-start.5 = (bf16[512,1024]{1,0:T(8,128)(2,1)}, bf16[512,1024]{1,0:T(8,128)(2,1)S(1)}, u32[]{:S(2)}, u32[]{:S(2)}) collective-permute-start(bf16[512,1024]{1,0:T(8,128)(2,1)} %transpose_w.1.refs_5_), channel_id=1, source_target_pairs={{0,128},{128,256},{256,384},{384,0},{1,129},{129,257},{257,385},{3... | collective-permute-start | bytes 3145736 | tf_op jit(solution)/shard_map/ppermute | solution.py:26
  6.7 3.4 %collective-permute-start.7 = (bf16[512,1024]{1,0:T(8,128)(2,1)}, bf16[512,1024]{1,0:T(8,128)(2,1)S(1)}, u32[]{:S(2)}, u32[]{:S(2)}) collective-permute-start(bf16[512,1024]{1,0:T(8,128)(2,1)} %transpose_w.1.refs_5_), channel_id=1, source_target_pairs={{0,384},{128,0},{256,128},{384,256},{1,385},{129,1},{257,129},{385... | collective-permute-start | bytes 3145736 | tf_op jit(solution)/shard_map/ppermute | solution.py:26
  10.1 2.1 %pack_kv.1 = bf16[8,2,2,128,128]{4,3,2,1,0:T(8,128)(2,1)} custom-call(bf16[2,128,1024]{2,1,0:T(8,128)(2,1)} %k_ref.1, bf16[2,128,1024]{2,1,0:T(8,128)(2,1)} %v_ref.1), custom_call_target="tpu_custom_call" | custom-call | tf_op jit(solution)/shard_map/pack_kv/pallas_call | solution.py:41
  12.2 11.6 %all-to-all-start = ((bf16[16,2,128,128]{3,2,1,0:T(8,128)(2,1)}), bf16[16,2,128,128]{3,2,1,0:T(8,128)(2,1)}, u32[]{:S(2)}, u32[]{:S(2)}) async-start(bf16[16,2,128,128]{3,2,1,0:T(8,128)(2,1)} %bitcast.9), calls=%async_computation | async-start | bytes 2097152 | tf_op jit(solution)/shard_map/all_to_all | solution.py:220
  23.8 0.0 copy-start.8
  23.8 7.2 %collective-permute-done.5.refs_7_ = bf16[512,1024]{1,0:T(8,128)(2,1)S(1)} collective-permute-done((bf16[512,1024]{1,0:T(8,128)(2,1)}, bf16[512,1024]{1,0:T(8,128)(2,1)S(1)}, u32[]{:S(2)}, u32[]{:S(2)}) %collective-permute-start.5) | collective-permute-done | bytes 1048608 | tf_op jit(solution)/shard_map/ppermute | solution.py:26
  31.0 1.6 collective-permute-done.7.refs_9_
  32.7 0.1 broadcast_select_fusion
  32.8 4.6 %collective-permute-start.9 = (bf16[512,1024]{1,0:T(8,128)(2,1)S(1)}, bf16[512,1024]{1,0:T(8,128)(2,1)}, u32[]{:S(2)}, u32[]{:S(2)}) collective-permute-start(bf16[512,1024]{1,0:T(8,128)(2,1)S(1)} %broadcast_select_fusion), channel_id=1, source_target_pairs={{0,128},{1,385},{128,256},{129,1},{256,384},{257,129},{384,0},{385... | collective-permute-start | bytes 3145736 | tf_op jit(solution)/shard_map/ppermute | solution.py:31
  37.4 2.4 %collective-permute-start.4 = (bf16[512,1024]{1,0:T(8,128)(2,1)S(1)}, bf16[512,1024]{1,0:T(8,128)(2,1)}, u32[]{:S(2)}, u32[]{:S(2)}) collective-permute-start(bf16[512,1024]{1,0:T(8,128)(2,1)S(1)} %copy-done), channel_id=1, source_target_pairs={{0,1},{1,0},{2,3},{3,2},{4,5},{5,4},{6,7},{7,6},{8,9},{9,8},{10,11... | collective-permute-start | bytes 3145736 | tf_op jit(solution)/shard_map/ppermute | solution.py:26
  39.8 1.9 collective-permute-start.6
  41.8 2.4 %collective-permute-start.8 = (bf16[512,1024]{1,0:T(8,128)(2,1)S(1)}, bf16[512,1024]{1,0:T(8,128)(2,1)}, u32[]{:S(2)}, u32[]{:S(2)}) collective-permute-start(bf16[512,1024]{1,0:T(8,128)(2,1)S(1)} %collective-permute-done.7.refs_9_), channel_id=1, source_target_pairs={{0,1},{1,0},{2,3},{3,2},{4,5},{5,4},{6,7},{7,6},{8,9},{9,8},{10,11... | collective-permute-start | bytes 3145736 | tf_op jit(solution)/shard_map/ppermute | solution.py:26
  44.2 4.9 %collective-permute-done.9.refs_11_ = bf16[512,1024]{1,0:T(8,128)(2,1)} collective-permute-done((bf16[512,1024]{1,0:T(8,128)(2,1)S(1)}, bf16[512,1024]{1,0:T(8,128)(2,1)}, u32[]{:S(2)}, u32[]{:S(2)}) %collective-permute-start.9) | collective-permute-done | bytes 1048608 | tf_op jit(solution)/shard_map/ppermute | solution.py:31
  49.1 5.3 %collective-permute-start.10 = (bf16[512,1024]{1,0:T(8,128)(2,1)}, bf16[512,1024]{1,0:T(8,128)(2,1)}, u32[]{:S(2)}, u32[]{:S(2)}) collective-permute-start(bf16[512,1024]{1,0:T(8,128)(2,1)} %collective-permute-done.9.refs_11_), channel_id=1, source_target_pairs={{0,1},{1,0},{2,3},{3,2},{4,5},{5,4},{6,7},{7,6},{8,9},{9,8},{10,11... | collective-permute-start | bytes 3145736 | tf_op jit(solution)/shard_map/ppermute | solution.py:26
  54.4 1.9 collective-permute-start
  56.4 0.6 pad_add_fusion.s_ref.refs_0_
  57.0 0.7 collective-permute-done.other_ref
  57.7 0.0 all-to-all-done.kv_ref
  57.7 0.7 copy-done.14
  58.3 8.2 %attend.1.refs_1_ = bf16[2,64,1024]{2,1,0:T(8,128)(2,1)} custom-call(s32[4]{0:T(128)} %pad_add_fusion.s_ref.refs_0_, s32[2]{0:T(128)} %cache_ref.1, s32[64]{0:T(128)} %length_ref.1, bf16[128,1024]{1,0:T(8,128)(2,1)} %mine_ref.1, bf16[64,1024]{1,0:T(8,128)(2,1)} %copy-done.14, bf16[16,2,128,128]{3,2,1,0:T(8,128)(2,1)} %all-to-all-done.kv_ref, ...), custom_call_target="tpu_custom_call" | custom-call | tf_op jit(solution)/shard_map/attend/pallas_call | solution.py:100
  66.5 3.2 %collective-permute-start.1 = (bf16[2,64,1024]{2,1,0:T(8,128)(2,1)}, bf16[2,64,1024]{2,1,0:T(8,128)(2,1)S(1)}, u32[]{:S(2)}, u32[]{:S(2)}) collective-permute-start(bf16[2,64,1024]{2,1,0:T(8,128)(2,1)} %attend.1.refs_1_), channel_id=1, source_target_pairs={{0,16},{16,32},{32,48},{48,64},{64,80},{80,96},{96,112},{112,0},{1... | collective-permute-start | bytes 786440 | tf_op jit(solution)/shard_map/ppermute | solution.py:26
  69.7 0.0 collective-permute-done.4.refs_6_
  69.7 2.1 collective-permute-start.2
  71.8 0.0 collective-permute-done.6.refs_8_
  71.8 5.3 %collective-permute-start.3 = (bf16[2,64,1024]{2,1,0:T(8,128)(2,1)}, bf16[2,64,1024]{2,1,0:T(8,128)(2,1)S(1)}, u32[]{:S(2)}, u32[]{:S(2)}) collective-permute-start(bf16[2,64,1024]{2,1,0:T(8,128)(2,1)} %attend.1.refs_1_), channel_id=1, source_target_pairs={{0,32},{16,48},{32,64},{48,80},{64,96},{80,112},{96,0},{112,16},{1... | collective-permute-start | bytes 786440 | tf_op jit(solution)/shard_map/ppermute | solution.py:26
  77.1 0.0 collective-permute-done.8.refs_10_
  77.1 0.0 collective-permute-done.1.refs_2_
  77.1 2.1 collective-permute-done.2.refs_3_
  79.2 5.6 %collective-permute-done.3.refs_4_ = bf16[2,64,1024]{2,1,0:T(8,128)(2,1)S(1)} collective-permute-done((bf16[2,64,1024]{2,1,0:T(8,128)(2,1)}, bf16[2,64,1024]{2,1,0:T(8,128)(2,1)S(1)}, u32[]{:S(2)}, u32[]{:S(2)}) %collective-permute-start.3) | collective-permute-done | bytes 262176 | tf_op jit(solution)/shard_map/ppermute | solution.py:26
  84.9 0.0 collective-permute-done.10.refs_12_
  84.9 0.6 broadcast_in_dim.3.refs_13_
  85.5 0.1 copy-done.5
  85.6 9.1 %project.2 = (bf16[4,8,32,512]{3,2,1,0:T(8,128)(2,1)}, f32[8,128]{1,0:T(8,128)}) custom-call(s32[4]{0:T(128)} %pad_add_fusion.s_ref.refs_0_, bf16[2,64,1024]{2,1,0:T(8,128)(2,1)} %attend.1.refs_1_, bf16[2,64,1024]{2,1,0:T(8,128)(2,1)} %copy-done.10, bf16[2,64,1024]{2,1,0:T(8,128)(2,1)} %copy-done.12, bf16[2,64,1024]{2,1,0:T(8,128)(2,1)} %copy-done.5, ...), custom_call_target="tpu_custom_call" | custom-call | tf_op jit(solution)/shard_map/project/pallas_call | solution.py:145
  94.7 11.8 %all-to-all-start.1 = ((bf16[32,32,512]{2,1,0:T(8,128)(2,1)}), bf16[32,32,512]{2,1,0:T(8,128)(2,1)S(1)}, u32[]{:S(2)}, u32[]{:S(2)}) async-start(bf16[32,32,512]{2,1,0:T(8,128)(2,1)} %bitcast.12), calls=%async_computation.1 | async-start | bytes 2097152 | tf_op jit(solution)/shard_map/all_to_all | solution.py:220
  106.5 4.1 %collective-permute-start.11 = (bf16[2,64,1024]{2,1,0:T(8,128)(2,1)S(1)}, bf16[2,64,1024]{2,1,0:T(8,128)(2,1)S(1)}, u32[]{:S(2)}, u32[]{:S(2)}) collective-permute-start(bf16[2,64,1024]{2,1,0:T(8,128)(2,1)S(1)} %copy-done.4), channel_id=1, source_target_pairs={{0,96},{16,112},{32,0},{48,16},{64,32},{80,48},{96,64},{112,80},{1... | collective-permute-start | bytes 786440 | tf_op jit(solution)/shard_map/ppermute | solution.py:26
  110.6 7.7 %collective-permute-start.12 = (bf16[2,64,1024]{2,1,0:T(8,128)(2,1)S(1)}, bf16[2,64,1024]{2,1,0:T(8,128)(2,1)S(1)}, u32[]{:S(2)}, u32[]{:S(2)}) collective-permute-start(bf16[2,64,1024]{2,1,0:T(8,128)(2,1)S(1)} %copy-done.6), channel_id=1, source_target_pairs={{0,16},{16,32},{32,48},{48,64},{64,80},{80,96},{96,112},{112,0},{1... | collective-permute-start | bytes 786440 | tf_op jit(solution)/shard_map/ppermute | solution.py:26
  118.3 9.7 %collective-permute-start.13 = (bf16[2,64,1024]{2,1,0:T(8,128)(2,1)S(1)}, bf16[2,64,1024]{2,1,0:T(8,128)(2,1)S(1)}, u32[]{:S(2)}, u32[]{:S(2)}) collective-permute-start(bf16[2,64,1024]{2,1,0:T(8,128)(2,1)S(1)} %collective-permute-done.11.refs_1_), channel_id=1, source_target_pairs={{0,112},{16,0},{32,16},{48,32},{64,48},{80,64},{96,80},{112,96},{1... | collective-permute-start | bytes 786440 | tf_op jit(solution)/shard_map/ppermute | solution.py:26
  128.0 4.2 %collective-permute-start.14 = (bf16[2,64,1024]{2,1,0:T(8,128)(2,1)S(1)}, bf16[2,64,1024]{2,1,0:T(8,128)(2,1)S(1)}, u32[]{:S(2)}, u32[]{:S(2)}) collective-permute-start(bf16[2,64,1024]{2,1,0:T(8,128)(2,1)S(1)} %broadcast_select_fusion.1), channel_id=1, source_target_pairs={{0,32},{1,97},{16,48},{17,113},{32,64},{33,1},{48,80},{49,17},{64,... | collective-permute-start | bytes 786440 | tf_op jit(solution)/shard_map/ppermute | solution.py:31
  132.2 1.2 collective-permute-done.13.refs_3_
  133.4 7.6 %collective-permute-done.14.refs_4_ = bf16[2,64,1024]{2,1,0:T(8,128)(2,1)S(1)} collective-permute-done((bf16[2,64,1024]{2,1,0:T(8,128)(2,1)S(1)}, bf16[2,64,1024]{2,1,0:T(8,128)(2,1)S(1)}, u32[]{:S(2)}, u32[]{:S(2)}) %collective-permute-start.14) | collective-permute-done | bytes 262176 | tf_op jit(solution)/shard_map/ppermute | solution.py:31
  141.1 0.7 copy-done.13
  141.8 9.1 %project.3 = (bf16[4,8,32,512]{3,2,1,0:T(8,128)(2,1)}, f32[8,128]{1,0:T(8,128)}) custom-call(s32[4]{0:T(128)} %pad_add_fusion.s_ref.refs_0_, bf16[2,64,1024]{2,1,0:T(8,128)(2,1)} %copy-done.7, bf16[2,64,1024]{2,1,0:T(8,128)(2,1)} %copy-done.9, bf16[2,64,1024]{2,1,0:T(8,128)(2,1)} %copy-done.11, bf16[2,64,1024]{2,1,0:T(8,128)(2,1)} %copy-done.13, ...), custom_call_target="tpu_custom_call" | custom-call | tf_op jit(solution)/shard_map/project/pallas_call | solution.py:145
  150.8 0.0 all-to-all-done.1
  150.9 34.5 %all_to_all.20 = bf16[32,32,512]{2,1,0:T(8,128)(2,1)} all-to-all(bf16[32,32,512]{2,1,0:T(8,128)(2,1)} %bitcast.13), channel_id=1, replica_groups=mesh['x'=4,'y'=8,'z'=8,'c'=2] {'x','z'}, dimensions={0} | all-to-all | bytes 2097152 | tf_op jit(solution)/shard_map/all_to_all | solution.py:220
  185.3 3.0 %place.1 = bf16[16,32,384]{2,1,0:T(8,128)(2,1)} custom-call(s32[4]{0:T(128)} %pad_add_fusion.s_ref.refs_0_, s32[64]{0:T(128)} %length_ref.1, s32[64]{0:T(128)} %group_ref.1, s32[64]{0:T(128)} %first_ref.1, bf16[4,8,32,512]{3,2,1,0:T(8,128)(2,1)} %bitcast.10, bf16[4,8,32,512]{3,2,1,0:T(8,128)(2,1)} %bitcast.11), custom_call_target="tpu_custom_call" | custom-call | tf_op jit(solution)/shard_map/place/pallas_call | solution.py:184
  188.3 22.9 %all_to_all.21.i_ref = bf16[16,32,384]{2,1,0:T(8,128)(2,1)} all-to-all(bf16[16,32,384]{2,1,0:T(8,128)(2,1)} %place.1), channel_id=1, replica_groups=mesh['x'=4,'y'=8,'z'=8,'c'=2] {'z','c'}, dimensions={0} | all-to-all | bytes 786432 | tf_op jit(solution)/shard_map/all_to_all | solution.py:220
  211.2 1.9 finish.1
  (30 shorter events, 0.1 us)
Async XLA Ops:
  3.6 27.5 %collective-permute-start.5 = (bf16[512,1024]{1,0:T(8,128)(2,1)}, bf16[512,1024]{1,0:T(8,128)(2,1)S(1)}, u32[]{:S(2)}, u32[]{:S(2)}) collective-permute-start(bf16[512,1024]{1,0:T(8,128)(2,1)} %transpose_w.1.refs_5_), channel_id=1, source_target_pairs={{0,128},{128,256},{256,384},{384,0},{1,129},{129,257},{257,385},{3... | collective-permute-start | bytes 3145736 | tf_op jit(solution)/shard_map/ppermute | solution.py:26
  6.7 26.0 %collective-permute-start.7 = (bf16[512,1024]{1,0:T(8,128)(2,1)}, bf16[512,1024]{1,0:T(8,128)(2,1)S(1)}, u32[]{:S(2)}, u32[]{:S(2)}) collective-permute-start(bf16[512,1024]{1,0:T(8,128)(2,1)} %transpose_w.1.refs_5_), channel_id=1, source_target_pairs={{0,384},{128,0},{256,128},{384,256},{1,385},{129,1},{257,129},{385... | collective-permute-start | bytes 3145736 | tf_op jit(solution)/shard_map/ppermute | solution.py:26
  12.2 45.5 %all-to-all-start = ((bf16[16,2,128,128]{3,2,1,0:T(8,128)(2,1)}), bf16[16,2,128,128]{3,2,1,0:T(8,128)(2,1)}, u32[]{:S(2)}, u32[]{:S(2)}) async-start(bf16[16,2,128,128]{3,2,1,0:T(8,128)(2,1)} %bitcast.9), calls=%async_computation | async-start | bytes 2097152 | tf_op jit(solution)/shard_map/all_to_all | solution.py:220
  23.8 13.6 %copy-start = (bf16[512,1024]{1,0:T(8,128)(2,1)S(1)}, bf16[512,1024]{1,0:T(8,128)(2,1)}, u32[]{:S(2)}) copy-start(bf16[512,1024]{1,0:T(8,128)(2,1)} %transpose_w.1.refs_5_) | copy-start | bytes 3145732
  23.8 30.6 %copy-start.8 = (bf16[128,1024]{1,0:T(8,128)(2,1)S(1)}, bf16[128,1024]{1,0:T(8,128)(2,1)}, u32[]{:S(2)}) copy-start(bf16[128,1024]{1,0:T(8,128)(2,1)} %mine_ref.1) | copy-start | bytes 786436
  31.0 8.8 %copy-start.1 = (bf16[512,1024]{1,0:T(8,128)(2,1)}, bf16[512,1024]{1,0:T(8,128)(2,1)S(1)}, u32[]{:S(2)}) copy-start(bf16[512,1024]{1,0:T(8,128)(2,1)S(1)} %collective-permute-done.5.refs_7_) | copy-start | bytes 3145732
  32.7 9.1 %copy-start.2 = (bf16[512,1024]{1,0:T(8,128)(2,1)}, bf16[512,1024]{1,0:T(8,128)(2,1)S(1)}, u32[]{:S(2)}) copy-start(bf16[512,1024]{1,0:T(8,128)(2,1)S(1)} %collective-permute-done.7.refs_9_) | copy-start | bytes 3145732
  32.8 16.3 %collective-permute-start.9 = (bf16[512,1024]{1,0:T(8,128)(2,1)S(1)}, bf16[512,1024]{1,0:T(8,128)(2,1)}, u32[]{:S(2)}, u32[]{:S(2)}) collective-permute-start(bf16[512,1024]{1,0:T(8,128)(2,1)S(1)} %broadcast_select_fusion), channel_id=1, source_target_pairs={{0,128},{1,385},{128,256},{129,1},{256,384},{257,129},{384,0},{385... | collective-permute-start | bytes 3145736 | tf_op jit(solution)/shard_map/ppermute | solution.py:31
  37.4 32.3 %collective-permute-start.4 = (bf16[512,1024]{1,0:T(8,128)(2,1)S(1)}, bf16[512,1024]{1,0:T(8,128)(2,1)}, u32[]{:S(2)}, u32[]{:S(2)}) collective-permute-start(bf16[512,1024]{1,0:T(8,128)(2,1)S(1)} %copy-done), channel_id=1, source_target_pairs={{0,1},{1,0},{2,3},{3,2},{4,5},{5,4},{6,7},{7,6},{8,9},{9,8},{10,11... | collective-permute-start | bytes 3145736 | tf_op jit(solution)/shard_map/ppermute | solution.py:26
  39.8 32.0 %collective-permute-start.6 = (bf16[512,1024]{1,0:T(8,128)(2,1)S(1)}, bf16[512,1024]{1,0:T(8,128)(2,1)}, u32[]{:S(2)}, u32[]{:S(2)}) collective-permute-start(bf16[512,1024]{1,0:T(8,128)(2,1)S(1)} %collective-permute-done.5.refs_7_), channel_id=1, source_target_pairs={{0,1},{1,0},{2,3},{3,2},{4,5},{5,4},{6,7},{7,6},{8,9},{9,8},{10,11... | collective-permute-start | bytes 3145736 | tf_op jit(solution)/shard_map/ppermute | solution.py:26
  41.8 35.3 %collective-permute-start.8 = (bf16[512,1024]{1,0:T(8,128)(2,1)S(1)}, bf16[512,1024]{1,0:T(8,128)(2,1)}, u32[]{:S(2)}, u32[]{:S(2)}) collective-permute-start(bf16[512,1024]{1,0:T(8,128)(2,1)S(1)} %collective-permute-done.7.refs_9_), channel_id=1, source_target_pairs={{0,1},{1,0},{2,3},{3,2},{4,5},{5,4},{6,7},{7,6},{8,9},{9,8},{10,11... | collective-permute-start | bytes 3145736 | tf_op jit(solution)/shard_map/ppermute | solution.py:26
  49.1 35.8 %collective-permute-start.10 = (bf16[512,1024]{1,0:T(8,128)(2,1)}, bf16[512,1024]{1,0:T(8,128)(2,1)}, u32[]{:S(2)}, u32[]{:S(2)}) collective-permute-start(bf16[512,1024]{1,0:T(8,128)(2,1)} %collective-permute-done.9.refs_11_), channel_id=1, source_target_pairs={{0,1},{1,0},{2,3},{3,2},{4,5},{5,4},{6,7},{7,6},{8,9},{9,8},{10,11... | collective-permute-start | bytes 3145736 | tf_op jit(solution)/shard_map/ppermute | solution.py:26
  54.4 3.2 %collective-permute-start = (bf16[64,1024]{1,0:T(8,128)(2,1)S(1)}, bf16[64,1024]{1,0:T(8,128)(2,1)S(1)}, u32[]{:S(2)}, u32[]{:S(2)}) collective-permute-start(bf16[64,1024]{1,0:T(8,128)(2,1)S(1)} %constant_dynamic-slice_fusion), channel_id=1, source_target_pairs={{0,1},{1,0},{2,3},{3,2},{4,5},{5,4},{6,7},{7,6},{8,9},{9,8},{10,11... | collective-permute-start | bytes 393224 | tf_op jit(solution)/shard_map/ppermute | solution.py:26
  57.7 0.7 copy-start.14
  66.5 10.6 %collective-permute-start.1 = (bf16[2,64,1024]{2,1,0:T(8,128)(2,1)}, bf16[2,64,1024]{2,1,0:T(8,128)(2,1)S(1)}, u32[]{:S(2)}, u32[]{:S(2)}) collective-permute-start(bf16[2,64,1024]{2,1,0:T(8,128)(2,1)} %attend.1.refs_1_), channel_id=1, source_target_pairs={{0,16},{16,32},{32,48},{48,64},{64,80},{80,96},{96,112},{112,0},{1... | collective-permute-start | bytes 786440 | tf_op jit(solution)/shard_map/ppermute | solution.py:26
  69.7 9.5 %collective-permute-start.2 = (bf16[2,64,1024]{2,1,0:T(8,128)(2,1)}, bf16[2,64,1024]{2,1,0:T(8,128)(2,1)S(1)}, u32[]{:S(2)}, u32[]{:S(2)}) collective-permute-start(bf16[2,64,1024]{2,1,0:T(8,128)(2,1)} %attend.1.refs_1_), channel_id=1, source_target_pairs={{0,112},{16,0},{32,16},{48,32},{64,48},{80,64},{96,80},{112,96},{1... | collective-permute-start | bytes 786440 | tf_op jit(solution)/shard_map/ppermute | solution.py:26
  71.8 13.1 %collective-permute-start.3 = (bf16[2,64,1024]{2,1,0:T(8,128)(2,1)}, bf16[2,64,1024]{2,1,0:T(8,128)(2,1)S(1)}, u32[]{:S(2)}, u32[]{:S(2)}) collective-permute-start(bf16[2,64,1024]{2,1,0:T(8,128)(2,1)} %attend.1.refs_1_), channel_id=1, source_target_pairs={{0,32},{16,48},{32,64},{48,80},{64,96},{80,112},{96,0},{112,16},{1... | collective-permute-start | bytes 786440 | tf_op jit(solution)/shard_map/ppermute | solution.py:26
  77.1 8.4 %copy-start.10 = (bf16[2,64,1024]{2,1,0:T(8,128)(2,1)}, bf16[2,64,1024]{2,1,0:T(8,128)(2,1)S(1)}, u32[]{:S(2)}) copy-start(bf16[2,64,1024]{2,1,0:T(8,128)(2,1)S(1)} %collective-permute-done.1.refs_2_) | copy-start | bytes 786436
  79.2 6.3 %copy-start.12 = (bf16[2,64,1024]{2,1,0:T(8,128)(2,1)}, bf16[2,64,1024]{2,1,0:T(8,128)(2,1)S(1)}, u32[]{:S(2)}) copy-start(bf16[2,64,1024]{2,1,0:T(8,128)(2,1)S(1)} %collective-permute-done.2.refs_3_) | copy-start | bytes 786436
  84.9 0.7 copy-start.5
  94.7 11.8 %copy-start.4 = (bf16[2,64,1024]{2,1,0:T(8,128)(2,1)S(1)}, bf16[2,64,1024]{2,1,0:T(8,128)(2,1)}, u32[]{:S(2)}) copy-start(bf16[2,64,1024]{2,1,0:T(8,128)(2,1)} %attend.1.refs_1_) | copy-start | bytes 786436
  94.7 15.9 %copy-start.6 = (bf16[2,64,1024]{2,1,0:T(8,128)(2,1)S(1)}, bf16[2,64,1024]{2,1,0:T(8,128)(2,1)}, u32[]{:S(2)}) copy-start(bf16[2,64,1024]{2,1,0:T(8,128)(2,1)} %copy-done.5) | copy-start | bytes 786436
  94.7 56.2 %all-to-all-start.1 = ((bf16[32,32,512]{2,1,0:T(8,128)(2,1)}), bf16[32,32,512]{2,1,0:T(8,128)(2,1)S(1)}, u32[]{:S(2)}, u32[]{:S(2)}) async-start(bf16[32,32,512]{2,1,0:T(8,128)(2,1)} %bitcast.12), calls=%async_computation.1 | async-start | bytes 2097152 | tf_op jit(solution)/shard_map/all_to_all | solution.py:220
  106.5 11.8 %collective-permute-start.11 = (bf16[2,64,1024]{2,1,0:T(8,128)(2,1)S(1)}, bf16[2,64,1024]{2,1,0:T(8,128)(2,1)S(1)}, u32[]{:S(2)}, u32[]{:S(2)}) collective-permute-start(bf16[2,64,1024]{2,1,0:T(8,128)(2,1)S(1)} %copy-done.4), channel_id=1, source_target_pairs={{0,96},{16,112},{32,0},{48,16},{64,32},{80,48},{96,64},{112,80},{1... | collective-permute-start | bytes 786440 | tf_op jit(solution)/shard_map/ppermute | solution.py:26
  110.6 21.6 %collective-permute-start.12 = (bf16[2,64,1024]{2,1,0:T(8,128)(2,1)S(1)}, bf16[2,64,1024]{2,1,0:T(8,128)(2,1)S(1)}, u32[]{:S(2)}, u32[]{:S(2)}) collective-permute-start(bf16[2,64,1024]{2,1,0:T(8,128)(2,1)S(1)} %copy-done.6), channel_id=1, source_target_pairs={{0,16},{16,32},{32,48},{48,64},{64,80},{80,96},{96,112},{112,0},{1... | collective-permute-start | bytes 786440 | tf_op jit(solution)/shard_map/ppermute | solution.py:26
  118.3 9.8 %copy-start.7 = (bf16[2,64,1024]{2,1,0:T(8,128)(2,1)}, bf16[2,64,1024]{2,1,0:T(8,128)(2,1)S(1)}, u32[]{:S(2)}) copy-start(bf16[2,64,1024]{2,1,0:T(8,128)(2,1)S(1)} %collective-permute-done.11.refs_1_) | copy-start | bytes 786436
  118.3 15.2 %collective-permute-start.13 = (bf16[2,64,1024]{2,1,0:T(8,128)(2,1)S(1)}, bf16[2,64,1024]{2,1,0:T(8,128)(2,1)S(1)}, u32[]{:S(2)}, u32[]{:S(2)}) collective-permute-start(bf16[2,64,1024]{2,1,0:T(8,128)(2,1)S(1)} %collective-permute-done.11.refs_1_), channel_id=1, source_target_pairs={{0,112},{16,0},{32,16},{48,32},{64,48},{80,64},{96,80},{112,96},{1... | collective-permute-start | bytes 786440 | tf_op jit(solution)/shard_map/ppermute | solution.py:26
  128.0 13.0 %collective-permute-start.14 = (bf16[2,64,1024]{2,1,0:T(8,128)(2,1)S(1)}, bf16[2,64,1024]{2,1,0:T(8,128)(2,1)S(1)}, u32[]{:S(2)}, u32[]{:S(2)}) collective-permute-start(bf16[2,64,1024]{2,1,0:T(8,128)(2,1)S(1)} %broadcast_select_fusion.1), channel_id=1, source_target_pairs={{0,32},{1,97},{16,48},{17,113},{32,64},{33,1},{48,80},{49,17},{64,... | collective-permute-start | bytes 786440 | tf_op jit(solution)/shard_map/ppermute | solution.py:31
  132.2 8.9 %copy-start.9 = (bf16[2,64,1024]{2,1,0:T(8,128)(2,1)}, bf16[2,64,1024]{2,1,0:T(8,128)(2,1)S(1)}, u32[]{:S(2)}) copy-start(bf16[2,64,1024]{2,1,0:T(8,128)(2,1)S(1)} %collective-permute-done.12.refs_2_) | copy-start | bytes 786436
  133.4 7.6 %copy-start.11 = (bf16[2,64,1024]{2,1,0:T(8,128)(2,1)}, bf16[2,64,1024]{2,1,0:T(8,128)(2,1)S(1)}, u32[]{:S(2)}) copy-start(bf16[2,64,1024]{2,1,0:T(8,128)(2,1)S(1)} %collective-permute-done.13.refs_3_) | copy-start | bytes 786436
  141.1 0.7 copy-start.13
  150.9 34.5 %copy-start.3 = (bf16[32,32,512]{2,1,0:T(8,128)(2,1)}, bf16[32,32,512]{2,1,0:T(8,128)(2,1)S(1)}, u32[]{:S(2)}) copy-start(bf16[32,32,512]{2,1,0:T(8,128)(2,1)S(1)} %all-to-all-done.1) | copy-start | bytes 3145732

commit v2 on v1

--- a/solution.py
+++ b/solution.py
@@ -11,6 +11,7 @@
 PACK = 96
 NX, NY, NZ = 4, 8, 8
 NEG_FILL = -1e30
+EXP2_SCALE = HEAD_DIM ** (-0.5) * 1.4426950408889634
 BF16 = jnp.bfloat16
 F32 = jnp.float32
 NT = (((1,), (1,)), ((), ()))
@@ -48,51 +49,35 @@
     )(k, v)
 
 
-def transpose_kernel(w_ref, o_ref):
-    o_ref[...] = w_ref[...].T
-
-
-def transpose(w):
-    return pl.pallas_call(
-        transpose_kernel,
-        grid=(4,),
-        in_specs=[pl.BlockSpec((1024, 128), lambda i: (0, i))],
-        out_specs=pl.BlockSpec((128, 1024), lambda i: (i, 0)),
-        out_shape=jax.ShapeDtypeStruct((512, 1024), BF16),
-        name="transpose_w",
-    )(w)
-
-
 def attend_kernel(s_ref, cache_ref, draft_ref, mine_ref, other_ref, kv_ref, dk_ref, dv_ref, o_ref):
     cache_len = cache_ref[s_ref[3]]
     draft_len = draft_ref[(s_ref[0] * NY + s_ref[1]) * 2 + s_ref[3]]
-    scale = HEAD_DIM ** (-0.5)
     keys = kv_ref[:, 0].reshape(2048, HEAD_DIM)
     values = kv_ref[:, 1].reshape(2048, HEAD_DIM)
     dk = dk_ref[...]
     dv = dv_ref[...]
     keep = lax.broadcasted_iota(jnp.int32, (1, 2048), 1) < cache_len
-    row = lax.broadcasted_iota(jnp.int32, (128, DRAFT), 0) % DRAFT
-    slot = lax.broadcasted_iota(jnp.int32, (128, DRAFT), 1)
+    row = lax.broadcasted_iota(jnp.int32, (256, DRAFT), 0) % DRAFT
+    slot = lax.broadcasted_iota(jnp.int32, (256, DRAFT), 1)
     keep_draft = (slot <= row) & (slot < draft_len)
-    live = lax.broadcasted_iota(jnp.int32, (128, 1), 0) % DRAFT < draft_len
+    live = lax.broadcasted_iota(jnp.int32, (256, 1), 0) % DRAFT < draft_len
     for side, q_ref in enumerate((mine_ref, other_ref)):
-        q = jnp.concatenate([q_ref[:, :HEAD_DIM], q_ref[:, HEAD_DIM:]], axis=0)
-        cached = lax.dot_general(q, keys, NT, preferred_element_type=F32) * scale
-        drafted = lax.dot_general(q, dk, NT, preferred_element_type=F32) * scale
+        q = jnp.concatenate([q_ref[:, h * HEAD_DIM : (h + 1) * HEAD_DIM] for h in range(4)], axis=0)
+        cached = lax.dot_general(q, keys, NT, preferred_element_type=F32)
+        drafted = lax.dot_general(q, dk, NT, preferred_element_type=F32)
         cached = jnp.where(keep, cached, NEG_FILL)
         drafted = jnp.where(keep_draft, drafted, NEG_FILL)
         high = jnp.maximum(
             jnp.max(cached, axis=1, keepdims=True), jnp.max(drafted, axis=1, keepdims=True)
         )
-        cached = jnp.exp(cached - high)
-        drafted = jnp.exp(drafted - high)
+        cached = jnp.exp2((cached - high) * EXP2_SCALE)
+        drafted = jnp.exp2((drafted - high) * EXP2_SCALE)
         total = jnp.sum(cached, axis=1, keepdims=True) + jnp.sum(drafted, axis=1, keepdims=True)
         mixed = jnp.dot(cached.astype(BF16), values, preferred_element_type=F32)
         mixed = mixed + jnp.dot(drafted.astype(BF16), dv, preferred_element_type=F32)
         mixed = jnp.where(live, mixed / total, 0.0).astype(BF16)
-        o_ref[side, :, :HEAD_DIM] = mixed[:DRAFT]
-        o_ref[side, :, HEAD_DIM:] = mixed[DRAFT:]
+        for h in range(4):
+            o_ref[side, :, h * HEAD_DIM : (h + 1) * HEAD_DIM] = mixed[h * DRAFT : (h + 1) * DRAFT]
 
 
 def attend(ids, cache_lengths, draft_lengths, q, other_q, kv, dk, dv):
@@ -101,15 +86,15 @@
         attend_kernel,
         grid_spec=pltpu.PrefetchScalarGridSpec(
             num_scalar_prefetch=3,
-            grid=(4,),
+            grid=(2,),
             in_specs=[
-                pl.BlockSpec((DRAFT, 256), lambda p, s, *_: (s[3], p)),
-                pl.BlockSpec((DRAFT, 256), lambda p, *_: (0, p)),
+                pl.BlockSpec((DRAFT, 512), lambda p, s, *_: (s[3], p)),
+                pl.BlockSpec((DRAFT, 512), lambda p, *_: (0, p)),
                 pl.BlockSpec((16, 2, 128, 128), lambda p, *_: (0, 0, 0, 0)),
                 draft,
                 draft,
             ],
-            out_specs=pl.BlockSpec((2, DRAFT, 256), lambda p, *_: (0, 0, p)),
+            out_specs=pl.BlockSpec((2, DRAFT, 512), lambda p, *_: (0, 0, p)),
         ),
         out_shape=jax.ShapeDtypeStruct((2, DRAFT, 1024), BF16),
         name="attend",
@@ -127,14 +112,14 @@
     a = jnp.concatenate([ref[0] for ref in rows], axis=0)
     b = jnp.concatenate([ref[1] for ref in rows], axis=0)
     for i, step in enumerate((0, -1, 1, 2)):
-        if i > 0 and 2 * i + 2 < 8:
+        if 0 < i < 3:
             copies[2 * i + 2].start()
             copies[2 * i + 3].start()
         copies[2 * i].wait()
         copies[2 * i + 1].wait()
-        acc = lax.dot_general(w_ref[2 * i], a, NT, preferred_element_type=F32)
-        acc = acc + lax.dot_general(w_ref[2 * i + 1], b, NT, preferred_element_type=F32)
-        acc = acc.astype(BF16).reshape(NZ, 2, 32, width)
+        acc = jnp.dot(a, w_ref[2 * i], preferred_element_type=F32)
+        acc = acc + jnp.dot(b, w_ref[2 * i + 1], preferred_element_type=F32)
+        acc = acc.astype(BF16).T.reshape(NZ, 2, 32, width)
         at = lax.rem(s_ref[0] + step + NX, NX)
         for half in range(2):
             o_ref[at, :, :, half * width : (half + 1) * width] = acc[:, half]
@@ -147,7 +132,7 @@
         in_specs=[SMEM] + [VMEM] * count + [pl.BlockSpec(memory_space=pltpu.HBM)] * 8 + [ANY],
         out_specs=[VMEM, VMEM],
         out_shape=[jax.ShapeDtypeStruct((NX, NZ, 32, 2 * count * DRAFT), BF16), TOKEN],
-        scratch_shapes=[pltpu.VMEM((8, 512, 1024), BF16), pltpu.SemaphoreType.DMA((8,))],
+        scratch_shapes=[pltpu.VMEM((8, 1024, 512), BF16), pltpu.SemaphoreType.DMA((8,))],
         name="project",
     )(ids, *rows, *weights, token)
 
@@ -237,11 +222,10 @@
 
     kv = exchange(pack_kv(cache_keys, cache_values).reshape(16, 2, 128, 128), ("z", "c"))
 
-    w0 = transpose(out_weight)
-    w1, w2 = shift(w0, "x", NX, 1), shift(w0, "x", NX, -1)
+    w1, w2 = shift(out_weight, "x", NX, 1), shift(out_weight, "x", NX, -1)
     w3 = shift_cores(jnp.where(c == 0, w1, w2), "x", NX, 1)
     weights = []
-    for w in (w0, w1, w2, w3):
+    for w in (out_weight, w1, w2, w3):
         weights += [w, shift(w, "c", 2, 1)]
     other_q = lax.dynamic_slice_in_dim(queries, (1 - c) * DRAFT, DRAFT, 0)
     other_q = shift(other_q, "c", 2, 1)

time: 214 us -> 207 us (0.967)
  Pallas kernels: 36.9 us -> 29.3 us
    pallas_call x1 -> x0, Pallas kernels: 3.57 us -> none  [transpose(): pl.pallas_call(transpose_kernel, grid=(4,), in_specs=[pl.BlockSpec((1024,...]
    pallas_call x2, Pallas kernels: 18.2 us -> 15.2 us  [project(): pl.pallas_call(lambda *refs: project_kernel(count, *refs), in_specs=[SMEM...]
  transfers between devices with their start and end apart: 17 -> 17, of which waited for: 8 -> 8; matrix products, arithmetic and copies ran while one was open for 0% -> 0% of each run, Pallas kernels for 9% -> 8%
where the time goes in v2:
time: 207 us; the launch traced here: 206 us
  starting transfers between devices  84.5 us (41%)
  blocking collectives  57.4 us (28%)
  waiting for transfers between devices  31.1 us (15%)
  Pallas kernels  29.3 us (14%)
  local copies, waits for them, and re-layouts  2.13 us (1%)
    all_to_all x2, blocking collectives, exchange(): return lax.all_to_all(value, axes, 0, 0, tiled=True)  57.4 us
    ppermute x13, starting transfers between devices, shift(): lax.ppermute(value, axis, [(i, (i + step) % size) for i in range(size)])  52.4 us
    all_to_all x2, starting transfers between devices, exchange(): return lax.all_to_all(value, axes, 0, 0, tiled=True)  23.3 us
    ppermute x13, waiting for transfers between devices, shift(): lax.ppermute(value, axis, [(i, (i + step) % size) for i in range(size)])  18.5 us
    pallas_call x2, Pallas kernels, project(): pl.pallas_call(lambda *refs: project_kernel(count, *refs), in_specs=[SMEM...  15.2 us
    ppermute x2, waiting for transfers between devices, shift_cores(): return lax.ppermute(value, (axis, 'c'), pairs)  12.5 us
    ppermute x2, starting transfers between devices, shift_cores(): return lax.ppermute(value, (axis, 'c'), pairs)  8.74 us
    pallas_call x1, Pallas kernels, attend(): pl.pallas_call(attend_kernel, grid_spec=pltpu.PrefetchScalarGridSpec(num_...  7.12 us
  transfers between devices with their start and end apart: 17, of which 8 were waited for; matrix products, arithmetic and copies ran while one was open for 0% of the time, Pallas kernels for 8%

profile of v2, /device:TPU:9, one launch (start us, length us, event | category | flops | bytes accessed | tf_op | source)
XLA Modules:
  0.0 205.5 jit_solution(5901356146785186015)
XLA Ops:
  0.0 3.1 %collective-permute-start.5 = (bf16[1024,512]{1,0:T(8,128)(2,1)}, bf16[1024,512]{1,0:T(8,128)(2,1)S(1)}, u32[]{:S(2)}, u32[]{:S(2)}) collective-permute-start(bf16[1024,512]{1,0:T(8,128)(2,1)} %refs_5_.3), channel_id=1, source_target_pairs={{0,128},{128,256},{256,384},{384,0},{1,129},{129,257},{257,385},{3... | collective-permute-start | bytes 3145736 | tf_op jit(solution)/shard_map/ppermute | solution.py:27
  3.1 3.4 %collective-permute-start.7 = (bf16[1024,512]{1,0:T(8,128)(2,1)}, bf16[1024,512]{1,0:T(8,128)(2,1)S(1)}, u32[]{:S(2)}, u32[]{:S(2)}) collective-permute-start(bf16[1024,512]{1,0:T(8,128)(2,1)} %refs_5_.3), channel_id=1, source_target_pairs={{0,384},{128,0},{256,128},{384,256},{1,385},{129,1},{257,129},{385... | collective-permute-start | bytes 3145736 | tf_op jit(solution)/shard_map/ppermute | solution.py:27
  6.5 2.2 %pack_kv.1 = bf16[8,2,2,128,128]{4,3,2,1,0:T(8,128)(2,1)} custom-call(bf16[2,128,1024]{2,1,0:T(8,128)(2,1)} %k_ref.1, bf16[2,128,1024]{2,1,0:T(8,128)(2,1)} %v_ref.1), custom_call_target="tpu_custom_call" | custom-call | tf_op jit(solution)/shard_map/pack_kv/pallas_call | solution.py:42
  8.7 11.6 %all-to-all-start = ((bf16[16,2,128,128]{3,2,1,0:T(8,128)(2,1)}), bf16[16,2,128,128]{3,2,1,0:T(8,128)(2,1)}, u32[]{:S(2)}, u32[]{:S(2)}) async-start(bf16[16,2,128,128]{3,2,1,0:T(8,128)(2,1)} %bitcast.9), calls=%async_computation | async-start | bytes 2097152 | tf_op jit(solution)/shard_map/all_to_all | solution.py:205
  20.2 0.0 copy-start.8
  20.2 7.2 %collective-permute-done.5.refs_7_ = bf16[1024,512]{1,0:T(8,128)(2,1)S(1)} collective-permute-done((bf16[1024,512]{1,0:T(8,128)(2,1)}, bf16[1024,512]{1,0:T(8,128)(2,1)S(1)}, u32[]{:S(2)}, u32[]{:S(2)}) %collective-permute-start.5) | collective-permute-done | bytes 1048608 | tf_op jit(solution)/shard_map/ppermute | solution.py:27
  27.5 1.6 collective-permute-done.7.refs_9_
  29.1 0.1 broadcast_select_fusion
  29.2 4.6 %collective-permute-start.9 = (bf16[1024,512]{1,0:T(8,128)(2,1)S(1)}, bf16[1024,512]{1,0:T(8,128)(2,1)}, u32[]{:S(2)}, u32[]{:S(2)}) collective-permute-start(bf16[1024,512]{1,0:T(8,128)(2,1)S(1)} %broadcast_select_fusion), channel_id=1, source_target_pairs={{0,128},{1,385},{128,256},{129,1},{256,384},{257,129},{384,0},{385... | collective-permute-start | bytes 3145736 | tf_op jit(solution)/shard_map/ppermute | solution.py:32
  33.8 2.4 %collective-permute-start.4 = (bf16[1024,512]{1,0:T(8,128)(2,1)S(1)}, bf16[1024,512]{1,0:T(8,128)(2,1)}, u32[]{:S(2)}, u32[]{:S(2)}) collective-permute-start(bf16[1024,512]{1,0:T(8,128)(2,1)S(1)} %copy-done.2), channel_id=1, source_target_pairs={{0,1},{1,0},{2,3},{3,2},{4,5},{5,4},{6,7},{7,6},{8,9},{9,8},{10,11... | collective-permute-start | bytes 3145736 | tf_op jit(solution)/shard_map/ppermute | solution.py:27
  36.3 1.9 collective-permute-start.6
  38.2 2.4 %collective-permute-start.8 = (bf16[1024,512]{1,0:T(8,128)(2,1)S(1)}, bf16[1024,512]{1,0:T(8,128)(2,1)}, u32[]{:S(2)}, u32[]{:S(2)}) collective-permute-start(bf16[1024,512]{1,0:T(8,128)(2,1)S(1)} %collective-permute-done.7.refs_9_), channel_id=1, source_target_pairs={{0,1},{1,0},{2,3},{3,2},{4,5},{5,4},{6,7},{7,6},{8,9},{9,8},{10,11... | collective-permute-start | bytes 3145736 | tf_op jit(solution)/shard_map/ppermute | solution.py:27
  40.6 4.9 %collective-permute-done.9.refs_11_ = bf16[1024,512]{1,0:T(8,128)(2,1)} collective-permute-done((bf16[1024,512]{1,0:T(8,128)(2,1)S(1)}, bf16[1024,512]{1,0:T(8,128)(2,1)}, u32[]{:S(2)}, u32[]{:S(2)}) %collective-permute-start.9) | collective-permute-done | bytes 1048608 | tf_op jit(solution)/shard_map/ppermute | solution.py:32
  45.5 5.3 %collective-permute-start.10 = (bf16[1024,512]{1,0:T(8,128)(2,1)}, bf16[1024,512]{1,0:T(8,128)(2,1)}, u32[]{:S(2)}, u32[]{:S(2)}) collective-permute-start(bf16[1024,512]{1,0:T(8,128)(2,1)} %collective-permute-done.9.refs_11_), channel_id=1, source_target_pairs={{0,1},{1,0},{2,3},{3,2},{4,5},{5,4},{6,7},{7,6},{8,9},{9,8},{10,11... | collective-permute-start | bytes 3145736 | tf_op jit(solution)/shard_map/ppermute | solution.py:27
  50.9 1.9 collective-permute-start
  52.8 0.6 pad_add_fusion.s_ref.refs_0_
  53.4 0.7 collective-permute-done.other_ref
  54.1 0.0 all-to-all-done.kv_ref
  54.1 0.7 copy-done.14
  54.8 7.1 %attend.1.refs_1_ = bf16[2,64,1024]{2,1,0:T(8,128)(2,1)} custom-call(s32[4]{0:T(128)} %pad_add_fusion.s_ref.refs_0_, s32[2]{0:T(128)} %cache_ref.1, s32[64]{0:T(128)} %length_ref.1, bf16[128,1024]{1,0:T(8,128)(2,1)} %mine_ref.1, bf16[64,1024]{1,0:T(8,128)(2,1)} %copy-done.14, bf16[16,2,128,128]{3,2,1,0:T(8,128)(2,1)} %all-to-all-done.kv_ref, ...), custom_call_target="tpu_custom_call" | custom-call | tf_op jit(solution)/shard_map/attend/pallas_call | solution.py:85
  61.9 3.2 %collective-permute-start.1 = (bf16[2,64,1024]{2,1,0:T(8,128)(2,1)}, bf16[2,64,1024]{2,1,0:T(8,128)(2,1)S(1)}, u32[]{:S(2)}, u32[]{:S(2)}) collective-permute-start(bf16[2,64,1024]{2,1,0:T(8,128)(2,1)} %attend.1.refs_1_), channel_id=1, source_target_pairs={{0,16},{16,32},{32,48},{48,64},{64,80},{80,96},{96,112},{112,0},{1... | collective-permute-start | bytes 786440 | tf_op jit(solution)/shard_map/ppermute | solution.py:27
  65.1 0.0 collective-permute-done.4.refs_6_
  65.1 2.1 %collective-permute-start.2 = (bf16[2,64,1024]{2,1,0:T(8,128)(2,1)}, bf16[2,64,1024]{2,1,0:T(8,128)(2,1)S(1)}, u32[]{:S(2)}, u32[]{:S(2)}) collective-permute-start(bf16[2,64,1024]{2,1,0:T(8,128)(2,1)} %attend.1.refs_1_), channel_id=1, source_target_pairs={{0,112},{16,0},{32,16},{48,32},{64,48},{80,64},{96,80},{112,96},{1... | collective-permute-start | bytes 786440 | tf_op jit(solution)/shard_map/ppermute | solution.py:27
  67.2 0.0 collective-permute-done.6.refs_8_
  67.2 5.3 %collective-permute-start.3 = (bf16[2,64,1024]{2,1,0:T(8,128)(2,1)}, bf16[2,64,1024]{2,1,0:T(8,128)(2,1)S(1)}, u32[]{:S(2)}, u32[]{:S(2)}) collective-permute-start(bf16[2,64,1024]{2,1,0:T(8,128)(2,1)} %attend.1.refs_1_), channel_id=1, source_target_pairs={{0,32},{16,48},{32,64},{48,80},{64,96},{80,112},{96,0},{112,16},{1... | collective-permute-start | bytes 786440 | tf_op jit(solution)/shard_map/ppermute | solution.py:27
  72.5 0.0 collective-permute-done.8.refs_10_
  72.5 0.0 collective-permute-done.1.refs_2_
  72.5 2.1 %collective-permute-done.2.refs_3_ = bf16[2,64,1024]{2,1,0:T(8,128)(2,1)S(1)} collective-permute-done((bf16[2,64,1024]{2,1,0:T(8,128)(2,1)}, bf16[2,64,1024]{2,1,0:T(8,128)(2,1)S(1)}, u32[]{:S(2)}, u32[]{:S(2)}) %collective-permute-start.2) | collective-permute-done | bytes 262176 | tf_op jit(solution)/shard_map/ppermute | solution.py:27
  74.6 5.6 %collective-permute-done.3.refs_4_ = bf16[2,64,1024]{2,1,0:T(8,128)(2,1)S(1)} collective-permute-done((bf16[2,64,1024]{2,1,0:T(8,128)(2,1)}, bf16[2,64,1024]{2,1,0:T(8,128)(2,1)S(1)}, u32[]{:S(2)}, u32[]{:S(2)}) %collective-permute-start.3) | collective-permute-done | bytes 262176 | tf_op jit(solution)/shard_map/ppermute | solution.py:27
  80.3 0.0 collective-permute-done.10.refs_12_
  80.3 0.6 broadcast_in_dim.3.refs_13_
  80.9 0.1 copy-done.5
  81.0 7.6 %project.2 = (bf16[4,8,32,512]{3,2,1,0:T(8,128)(2,1)}, f32[8,128]{1,0:T(8,128)}) custom-call(s32[4]{0:T(128)} %pad_add_fusion.s_ref.refs_0_, bf16[2,64,1024]{2,1,0:T(8,128)(2,1)} %attend.1.refs_1_, bf16[2,64,1024]{2,1,0:T(8,128)(2,1)} %copy-done.10, bf16[2,64,1024]{2,1,0:T(8,128)(2,1)} %copy-done.12, bf16[2,64,1024]{2,1,0:T(8,128)(2,1)} %copy-done.5, ...), custom_call_target="tpu_custom_call" | custom-call | tf_op jit(solution)/shard_map/project/pallas_call | solution.py:130
  88.6 11.8 %all-to-all-start.1 = ((bf16[32,32,512]{2,1,0:T(8,128)(2,1)}), bf16[32,32,512]{2,1,0:T(8,128)(2,1)S(1)}, u32[]{:S(2)}, u32[]{:S(2)}) async-start(bf16[32,32,512]{2,1,0:T(8,128)(2,1)} %bitcast.12), calls=%async_computation.1 | async-start | bytes 2097152 | tf_op jit(solution)/shard_map/all_to_all | solution.py:205
  100.4 4.1 %collective-permute-start.11 = (bf16[2,64,1024]{2,1,0:T(8,128)(2,1)S(1)}, bf16[2,64,1024]{2,1,0:T(8,128)(2,1)S(1)}, u32[]{:S(2)}, u32[]{:S(2)}) collective-permute-start(bf16[2,64,1024]{2,1,0:T(8,128)(2,1)S(1)} %copy-done.4), channel_id=1, source_target_pairs={{0,96},{16,112},{32,0},{48,16},{64,32},{80,48},{96,64},{112,80},{1... | collective-permute-start | bytes 786440 | tf_op jit(solution)/shard_map/ppermute | solution.py:27
  104.5 7.7 %collective-permute-start.12 = (bf16[2,64,1024]{2,1,0:T(8,128)(2,1)S(1)}, bf16[2,64,1024]{2,1,0:T(8,128)(2,1)S(1)}, u32[]{:S(2)}, u32[]{:S(2)}) collective-permute-start(bf16[2,64,1024]{2,1,0:T(8,128)(2,1)S(1)} %copy-done.6), channel_id=1, source_target_pairs={{0,16},{16,32},{32,48},{48,64},{64,80},{80,96},{96,112},{112,0},{1... | collective-permute-start | bytes 786440 | tf_op jit(solution)/shard_map/ppermute | solution.py:27
  112.2 0.0 collective-permute-done.11.refs_1_
  112.2 9.7 %collective-permute-start.13 = (bf16[2,64,1024]{2,1,0:T(8,128)(2,1)S(1)}, bf16[2,64,1024]{2,1,0:T(8,128)(2,1)S(1)}, u32[]{:S(2)}, u32[]{:S(2)}) collective-permute-start(bf16[2,64,1024]{2,1,0:T(8,128)(2,1)S(1)} %collective-permute-done.11.refs_1_), channel_id=1, source_target_pairs={{0,112},{16,0},{32,16},{48,32},{64,48},{80,64},{96,80},{112,96},{1... | collective-permute-start | bytes 786440 | tf_op jit(solution)/shard_map/ppermute | solution.py:27
  122.0 4.2 %collective-permute-start.14 = (bf16[2,64,1024]{2,1,0:T(8,128)(2,1)S(1)}, bf16[2,64,1024]{2,1,0:T(8,128)(2,1)S(1)}, u32[]{:S(2)}, u32[]{:S(2)}) collective-permute-start(bf16[2,64,1024]{2,1,0:T(8,128)(2,1)S(1)} %broadcast_select_fusion.1), channel_id=1, source_target_pairs={{0,32},{1,97},{16,48},{17,113},{32,64},{33,1},{48,80},{49,17},{64,... | collective-permute-start | bytes 786440 | tf_op jit(solution)/shard_map/ppermute | solution.py:32
  126.1 1.2 collective-permute-done.13.refs_3_
  127.4 7.6 %collective-permute-done.14.refs_4_ = bf16[2,64,1024]{2,1,0:T(8,128)(2,1)S(1)} collective-permute-done((bf16[2,64,1024]{2,1,0:T(8,128)(2,1)S(1)}, bf16[2,64,1024]{2,1,0:T(8,128)(2,1)S(1)}, u32[]{:S(2)}, u32[]{:S(2)}) %collective-permute-start.14) | collective-permute-done | bytes 262176 | tf_op jit(solution)/shard_map/ppermute | solution.py:32
  135.0 0.7 copy-done.13
  135.7 7.6 %project.3 = (bf16[4,8,32,512]{3,2,1,0:T(8,128)(2,1)}, f32[8,128]{1,0:T(8,128)}) custom-call(s32[4]{0:T(128)} %pad_add_fusion.s_ref.refs_0_, bf16[2,64,1024]{2,1,0:T(8,128)(2,1)} %copy-done.7, bf16[2,64,1024]{2,1,0:T(8,128)(2,1)} %copy-done.9, bf16[2,64,1024]{2,1,0:T(8,128)(2,1)} %copy-done.11, bf16[2,64,1024]{2,1,0:T(8,128)(2,1)} %copy-done.13, ...), custom_call_target="tpu_custom_call" | custom-call | tf_op jit(solution)/shard_map/project/pallas_call | solution.py:130
  143.3 0.0 all-to-all-done.1
  143.3 34.5 %all_to_all.20 = bf16[32,32,512]{2,1,0:T(8,128)(2,1)} all-to-all(bf16[32,32,512]{2,1,0:T(8,128)(2,1)} %bitcast.13), channel_id=1, replica_groups=mesh['x'=4,'y'=8,'z'=8,'c'=2] {'x','z'}, dimensions={0} | all-to-all | bytes 2097152 | tf_op jit(solution)/shard_map/all_to_all | solution.py:205
  177.8 3.0 %place.1 = bf16[16,32,384]{2,1,0:T(8,128)(2,1)} custom-call(s32[4]{0:T(128)} %pad_add_fusion.s_ref.refs_0_, s32[64]{0:T(128)} %length_ref.1, s32[64]{0:T(128)} %group_ref.1, s32[64]{0:T(128)} %first_ref.1, bf16[4,8,32,512]{3,2,1,0:T(8,128)(2,1)} %bitcast.10, bf16[4,8,32,512]{3,2,1,0:T(8,128)(2,1)} %bitcast.11), custom_call_target="tpu_custom_call" | custom-call | tf_op jit(solution)/shard_map/place/pallas_call | solution.py:169
  180.8 22.9 %all_to_all.21.i_ref = bf16[16,32,384]{2,1,0:T(8,128)(2,1)} all-to-all(bf16[16,32,384]{2,1,0:T(8,128)(2,1)} %place.1), channel_id=1, replica_groups=mesh['x'=4,'y'=8,'z'=8,'c'=2] {'z','c'}, dimensions={0} | all-to-all | bytes 786432 | tf_op jit(solution)/shard_map/all_to_all | solution.py:205
  203.6 1.9 finish.1
  (29 shorter events, 0.1 us)
Async XLA Ops:
  0.0 27.5 %collective-permute-start.5 = (bf16[1024,512]{1,0:T(8,128)(2,1)}, bf16[1024,512]{1,0:T(8,128)(2,1)S(1)}, u32[]{:S(2)}, u32[]{:S(2)}) collective-permute-start(bf16[1024,512]{1,0:T(8,128)(2,1)} %refs_5_.3), channel_id=1, source_target_pairs={{0,128},{128,256},{256,384},{384,0},{1,129},{129,257},{257,385},{3... | collective-permute-start | bytes 3145736 | tf_op jit(solution)/shard_map/ppermute | solution.py:27
  3.1 26.0 %collective-permute-start.7 = (bf16[1024,512]{1,0:T(8,128)(2,1)}, bf16[1024,512]{1,0:T(8,128)(2,1)S(1)}, u32[]{:S(2)}, u32[]{:S(2)}) collective-permute-start(bf16[1024,512]{1,0:T(8,128)(2,1)} %refs_5_.3), channel_id=1, source_target_pairs={{0,384},{128,0},{256,128},{384,256},{1,385},{129,1},{257,129},{385... | collective-permute-start | bytes 3145736 | tf_op jit(solution)/shard_map/ppermute | solution.py:27
  8.7 45.4 %all-to-all-start = ((bf16[16,2,128,128]{3,2,1,0:T(8,128)(2,1)}), bf16[16,2,128,128]{3,2,1,0:T(8,128)(2,1)}, u32[]{:S(2)}, u32[]{:S(2)}) async-start(bf16[16,2,128,128]{3,2,1,0:T(8,128)(2,1)} %bitcast.9), calls=%async_computation | async-start | bytes 2097152 | tf_op jit(solution)/shard_map/all_to_all | solution.py:205
  20.2 13.6 %copy-start.2 = (bf16[1024,512]{1,0:T(8,128)(2,1)S(1)}, bf16[1024,512]{1,0:T(8,128)(2,1)}, u32[]{:S(2)}) copy-start(bf16[1024,512]{1,0:T(8,128)(2,1)} %refs_5_.3) | copy-start | bytes 3145732
  20.2 30.6 %copy-start.8 = (bf16[128,1024]{1,0:T(8,128)(2,1)S(1)}, bf16[128,1024]{1,0:T(8,128)(2,1)}, u32[]{:S(2)}) copy-start(bf16[128,1024]{1,0:T(8,128)(2,1)} %mine_ref.1) | copy-start | bytes 786436
  27.5 8.8 %copy-start = (bf16[1024,512]{1,0:T(8,128)(2,1)}, bf16[1024,512]{1,0:T(8,128)(2,1)S(1)}, u32[]{:S(2)}) copy-start(bf16[1024,512]{1,0:T(8,128)(2,1)S(1)} %collective-permute-done.5.refs_7_) | copy-start | bytes 3145732
  29.1 9.1 %copy-start.1 = (bf16[1024,512]{1,0:T(8,128)(2,1)}, bf16[1024,512]{1,0:T(8,128)(2,1)S(1)}, u32[]{:S(2)}) copy-start(bf16[1024,512]{1,0:T(8,128)(2,1)S(1)} %collective-permute-done.7.refs_9_) | copy-start | bytes 3145732
  29.2 16.3 %collective-permute-start.9 = (bf16[1024,512]{1,0:T(8,128)(2,1)S(1)}, bf16[1024,512]{1,0:T(8,128)(2,1)}, u32[]{:S(2)}, u32[]{:S(2)}) collective-permute-start(bf16[1024,512]{1,0:T(8,128)(2,1)S(1)} %broadcast_select_fusion), channel_id=1, source_target_pairs={{0,128},{1,385},{128,256},{129,1},{256,384},{257,129},{384,0},{385... | collective-permute-start | bytes 3145736 | tf_op jit(solution)/shard_map/ppermute | solution.py:32
  33.8 31.3 %collective-permute-start.4 = (bf16[1024,512]{1,0:T(8,128)(2,1)S(1)}, bf16[1024,512]{1,0:T(8,128)(2,1)}, u32[]{:S(2)}, u32[]{:S(2)}) collective-permute-start(bf16[1024,512]{1,0:T(8,128)(2,1)S(1)} %copy-done.2), channel_id=1, source_target_pairs={{0,1},{1,0},{2,3},{3,2},{4,5},{5,4},{6,7},{7,6},{8,9},{9,8},{10,11... | collective-permute-start | bytes 3145736 | tf_op jit(solution)/shard_map/ppermute | solution.py:27
  36.3 30.9 %collective-permute-start.6 = (bf16[1024,512]{1,0:T(8,128)(2,1)S(1)}, bf16[1024,512]{1,0:T(8,128)(2,1)}, u32[]{:S(2)}, u32[]{:S(2)}) collective-permute-start(bf16[1024,512]{1,0:T(8,128)(2,1)S(1)} %collective-permute-done.5.refs_7_), channel_id=1, source_target_pairs={{0,1},{1,0},{2,3},{3,2},{4,5},{5,4},{6,7},{7,6},{8,9},{9,8},{10,11... | collective-permute-start | bytes 3145736 | tf_op jit(solution)/shard_map/ppermute | solution.py:27
  38.2 34.3 %collective-permute-start.8 = (bf16[1024,512]{1,0:T(8,128)(2,1)S(1)}, bf16[1024,512]{1,0:T(8,128)(2,1)}, u32[]{:S(2)}, u32[]{:S(2)}) collective-permute-start(bf16[1024,512]{1,0:T(8,128)(2,1)S(1)} %collective-permute-done.7.refs_9_), channel_id=1, source_target_pairs={{0,1},{1,0},{2,3},{3,2},{4,5},{5,4},{6,7},{7,6},{8,9},{9,8},{10,11... | collective-permute-start | bytes 3145736 | tf_op jit(solution)/shard_map/ppermute | solution.py:27
  45.5 34.7 %collective-permute-start.10 = (bf16[1024,512]{1,0:T(8,128)(2,1)}, bf16[1024,512]{1,0:T(8,128)(2,1)}, u32[]{:S(2)}, u32[]{:S(2)}) collective-permute-start(bf16[1024,512]{1,0:T(8,128)(2,1)} %collective-permute-done.9.refs_11_), channel_id=1, source_target_pairs={{0,1},{1,0},{2,3},{3,2},{4,5},{5,4},{6,7},{7,6},{8,9},{9,8},{10,11... | collective-permute-start | bytes 3145736 | tf_op jit(solution)/shard_map/ppermute | solution.py:27
  50.9 3.2 %collective-permute-start = (bf16[64,1024]{1,0:T(8,128)(2,1)S(1)}, bf16[64,1024]{1,0:T(8,128)(2,1)S(1)}, u32[]{:S(2)}, u32[]{:S(2)}) collective-permute-start(bf16[64,1024]{1,0:T(8,128)(2,1)S(1)} %constant_dynamic-slice_fusion), channel_id=1, source_target_pairs={{0,1},{1,0},{2,3},{3,2},{4,5},{5,4},{6,7},{7,6},{8,9},{9,8},{10,11... | collective-permute-start | bytes 393224 | tf_op jit(solution)/shard_map/ppermute | solution.py:27
  54.1 0.7 copy-start.14
  61.9 10.6 %collective-permute-start.1 = (bf16[2,64,1024]{2,1,0:T(8,128)(2,1)}, bf16[2,64,1024]{2,1,0:T(8,128)(2,1)S(1)}, u32[]{:S(2)}, u32[]{:S(2)}) collective-permute-start(bf16[2,64,1024]{2,1,0:T(8,128)(2,1)} %attend.1.refs_1_), channel_id=1, source_target_pairs={{0,16},{16,32},{32,48},{48,64},{64,80},{80,96},{96,112},{112,0},{1... | collective-permute-start | bytes 786440 | tf_op jit(solution)/shard_map/ppermute | solution.py:27
  65.1 9.5 %collective-permute-start.2 = (bf16[2,64,1024]{2,1,0:T(8,128)(2,1)}, bf16[2,64,1024]{2,1,0:T(8,128)(2,1)S(1)}, u32[]{:S(2)}, u32[]{:S(2)}) collective-permute-start(bf16[2,64,1024]{2,1,0:T(8,128)(2,1)} %attend.1.refs_1_), channel_id=1, source_target_pairs={{0,112},{16,0},{32,16},{48,32},{64,48},{80,64},{96,80},{112,96},{1... | collective-permute-start | bytes 786440 | tf_op jit(solution)/shard_map/ppermute | solution.py:27
  67.2 13.1 %collective-permute-start.3 = (bf16[2,64,1024]{2,1,0:T(8,128)(2,1)}, bf16[2,64,1024]{2,1,0:T(8,128)(2,1)S(1)}, u32[]{:S(2)}, u32[]{:S(2)}) collective-permute-start(bf16[2,64,1024]{2,1,0:T(8,128)(2,1)} %attend.1.refs_1_), channel_id=1, source_target_pairs={{0,32},{16,48},{32,64},{48,80},{64,96},{80,112},{96,0},{112,16},{1... | collective-permute-start | bytes 786440 | tf_op jit(solution)/shard_map/ppermute | solution.py:27
  72.5 8.4 %copy-start.10 = (bf16[2,64,1024]{2,1,0:T(8,128)(2,1)}, bf16[2,64,1024]{2,1,0:T(8,128)(2,1)S(1)}, u32[]{:S(2)}) copy-start(bf16[2,64,1024]{2,1,0:T(8,128)(2,1)S(1)} %collective-permute-done.1.refs_2_) | copy-start | bytes 786436
  74.6 6.2 %copy-start.12 = (bf16[2,64,1024]{2,1,0:T(8,128)(2,1)}, bf16[2,64,1024]{2,1,0:T(8,128)(2,1)S(1)}, u32[]{:S(2)}) copy-start(bf16[2,64,1024]{2,1,0:T(8,128)(2,1)S(1)} %collective-permute-done.2.refs_3_) | copy-start | bytes 786436
  80.3 0.7 copy-start.5
  88.6 11.8 %copy-start.4 = (bf16[2,64,1024]{2,1,0:T(8,128)(2,1)S(1)}, bf16[2,64,1024]{2,1,0:T(8,128)(2,1)}, u32[]{:S(2)}) copy-start(bf16[2,64,1024]{2,1,0:T(8,128)(2,1)} %attend.1.refs_1_) | copy-start | bytes 786436
  88.6 15.9 %copy-start.6 = (bf16[2,64,1024]{2,1,0:T(8,128)(2,1)S(1)}, bf16[2,64,1024]{2,1,0:T(8,128)(2,1)}, u32[]{:S(2)}) copy-start(bf16[2,64,1024]{2,1,0:T(8,128)(2,1)} %copy-done.5) | copy-start | bytes 786436
  88.6 54.6 %all-to-all-start.1 = ((bf16[32,32,512]{2,1,0:T(8,128)(2,1)}), bf16[32,32,512]{2,1,0:T(8,128)(2,1)S(1)}, u32[]{:S(2)}, u32[]{:S(2)}) async-start(bf16[32,32,512]{2,1,0:T(8,128)(2,1)} %bitcast.12), calls=%async_computation.1 | async-start | bytes 2097152 | tf_op jit(solution)/shard_map/all_to_all | solution.py:205
  100.4 11.8 %collective-permute-start.11 = (bf16[2,64,1024]{2,1,0:T(8,128)(2,1)S(1)}, bf16[2,64,1024]{2,1,0:T(8,128)(2,1)S(1)}, u32[]{:S(2)}, u32[]{:S(2)}) collective-permute-start(bf16[2,64,1024]{2,1,0:T(8,128)(2,1)S(1)} %copy-done.4), channel_id=1, source_target_pairs={{0,96},{16,112},{32,0},{48,16},{64,32},{80,48},{96,64},{112,80},{1... | collective-permute-start | bytes 786440 | tf_op jit(solution)/shard_map/ppermute | solution.py:27
  104.5 21.6 %collective-permute-start.12 = (bf16[2,64,1024]{2,1,0:T(8,128)(2,1)S(1)}, bf16[2,64,1024]{2,1,0:T(8,128)(2,1)S(1)}, u32[]{:S(2)}, u32[]{:S(2)}) collective-permute-start(bf16[2,64,1024]{2,1,0:T(8,128)(2,1)S(1)} %copy-done.6), channel_id=1, source_target_pairs={{0,16},{16,32},{32,48},{48,64},{64,80},{80,96},{96,112},{112,0},{1... | collective-permute-start | bytes 786440 | tf_op jit(solution)/shard_map/ppermute | solution.py:27
  112.2 9.8 %copy-start.7 = (bf16[2,64,1024]{2,1,0:T(8,128)(2,1)}, bf16[2,64,1024]{2,1,0:T(8,128)(2,1)S(1)}, u32[]{:S(2)}) copy-start(bf16[2,64,1024]{2,1,0:T(8,128)(2,1)S(1)} %collective-permute-done.11.refs_1_) | copy-start | bytes 786436
  112.2 15.2 %collective-permute-start.13 = (bf16[2,64,1024]{2,1,0:T(8,128)(2,1)S(1)}, bf16[2,64,1024]{2,1,0:T(8,128)(2,1)S(1)}, u32[]{:S(2)}, u32[]{:S(2)}) collective-permute-start(bf16[2,64,1024]{2,1,0:T(8,128)(2,1)S(1)} %collective-permute-done.11.refs_1_), channel_id=1, source_target_pairs={{0,112},{16,0},{32,16},{48,32},{64,48},{80,64},{96,80},{112,96},{1... | collective-permute-start | bytes 786440 | tf_op jit(solution)/shard_map/ppermute | solution.py:27
  122.0 13.0 %collective-permute-start.14 = (bf16[2,64,1024]{2,1,0:T(8,128)(2,1)S(1)}, bf16[2,64,1024]{2,1,0:T(8,128)(2,1)S(1)}, u32[]{:S(2)}, u32[]{:S(2)}) collective-permute-start(bf16[2,64,1024]{2,1,0:T(8,128)(2,1)S(1)} %broadcast_select_fusion.1), channel_id=1, source_target_pairs={{0,32},{1,97},{16,48},{17,113},{32,64},{33,1},{48,80},{49,17},{64,... | collective-permute-start | bytes 786440 | tf_op jit(solution)/shard_map/ppermute | solution.py:32
  126.1 8.9 %copy-start.9 = (bf16[2,64,1024]{2,1,0:T(8,128)(2,1)}, bf16[2,64,1024]{2,1,0:T(8,128)(2,1)S(1)}, u32[]{:S(2)}) copy-start(bf16[2,64,1024]{2,1,0:T(8,128)(2,1)S(1)} %collective-permute-done.12.refs_2_) | copy-start | bytes 786436
  127.4 7.6 %copy-start.11 = (bf16[2,64,1024]{2,1,0:T(8,128)(2,1)}, bf16[2,64,1024]{2,1,0:T(8,128)(2,1)S(1)}, u32[]{:S(2)}) copy-start(bf16[2,64,1024]{2,1,0:T(8,128)(2,1)S(1)} %collective-permute-done.13.refs_3_) | copy-start | bytes 786436
  135.0 0.7 copy-start.13
  143.3 34.5 %copy-start.3 = (bf16[32,32,512]{2,1,0:T(8,128)(2,1)}, bf16[32,32,512]{2,1,0:T(8,128)(2,1)S(1)}, u32[]{:S(2)}) copy-start(bf16[32,32,512]{2,1,0:T(8,128)(2,1)S(1)} %all-to-all-done.1) | copy-start | bytes 3145732

commit v3 on v2

--- a/solution.py
+++ b/solution.py
@@ -20,7 +20,7 @@
 ANY = pl.BlockSpec(memory_space=pl.ANY)
 TOKEN = jax.ShapeDtypeStruct((8, 128), F32)
 
-CHUNKS = ((0, -1, 1, -2), (2, -3, 3, -4))
+CHUNKS = ((0, -1, 1, -2, 2, -3, 3, -4),)
 
 
 def shift(value, axis, size, step):
@@ -232,9 +232,9 @@
 
     rows = attend(ids, cache_lengths, draft_lengths, queries, other_q, kv, draft_keys, draft_values)
     up1, down1 = shift(rows, "y", NY, 1), shift(rows, "y", NY, -1)
-    up2, down2 = shift(rows, "y", NY, 2), shift(rows, "y", NY, -2)
+    up2, down2 = shift(up1, "y", NY, 1), shift(down1, "y", NY, -1)
     up3, down3 = shift(up2, "y", NY, 1), shift(down2, "y", NY, -1)
-    far = shift_cores(jnp.where(c == 0, up2, down2), "y", NY, 2)
+    far = shift_cores(jnp.where(c == 0, up3, down3), "y", NY, 1)
     arrived = {0: rows, -1: up1, 1: down1, -2: up2, 2: down2, -3: up3, 3: down3, -4: far}
 
     token = jnp.zeros(TOKEN.shape, F32)

time: 207 us -> 215 us (1.039)
  the two profiles are of different devices: /device:TPU:9 before, /device:TPU:1 now
where the time goes in v3:
time: 215 us; the launch traced here: 214 us
  blocking collectives  79.7 us (37%)
  starting transfers between devices  58.4 us (27%)
  waiting for transfers between devices  44.4 us (21%)
  Pallas kernels  23.9 us (11%)
  local copies, waits for them, and re-layouts  4.97 us (2%)
    all_to_all x2, blocking collectives, exchange(): return lax.all_to_all(value, axes, 0, 0, tiled=True)  79.7 us
    ppermute x13, waiting for transfers between devices, shift(): lax.ppermute(value, axis, [(i, (i + step) % size) for i in range(size)])  41.4 us
    ppermute x13, starting transfers between devices, shift(): lax.ppermute(value, axis, [(i, (i + step) % size) for i in range(size)])  38.9 us
    all_to_all x1, starting transfers between devices, exchange(): return lax.all_to_all(value, axes, 0, 0, tiled=True)  11.8 us
    pallas_call x1, Pallas kernels, project(): pl.pallas_call(lambda *refs: project_kernel(count, *refs), in_specs=[SMEM...  9.77 us
    ppermute x2, starting transfers between devices, shift_cores(): return lax.ppermute(value, (axis, 'c'), pairs)  7.66 us
    pallas_call x1, Pallas kernels, attend(): pl.pallas_call(attend_kernel, grid_spec=pltpu.PrefetchScalarGridSpec(num_...  7.12 us
    unnamed x32, local copies, waits for them, and re-layouts  4.36 us
  transfers between devices with their start and end apart: 16, of which 7 were waited for; matrix products, arithmetic and copies ran while one was open for 1% of the time, Pallas kernels for 3%

profile of v3, /device:TPU:1, one launch (start us, length us, event | category | flops | bytes accessed | tf_op | source)
XLA Modules:
  0.0 213.6 jit_solution(16997214485198235659)
XLA Ops:
  0.0 2.1 pack_kv.1
  2.1 11.8 %all-to-all-start = ((bf16[16,2,128,128]{3,2,1,0:T(8,128)(2,1)}), bf16[16,2,128,128]{3,2,1,0:T(8,128)(2,1)S(1)}, u32[]{:S(2)}, u32[]{:S(2)}) async-start(bf16[16,2,128,128]{3,2,1,0:T(8,128)(2,1)} %bitcast.8), calls=%async_computation | async-start | bytes 2097152 | tf_op jit(solution)/shard_map/all_to_all | solution.py:205
  13.9 3.3 %collective-permute-start.9 = (bf16[1024,512]{1,0:T(8,128)(2,1)}, bf16[1024,512]{1,0:T(8,128)(2,1)S(1)}, u32[]{:S(2)}, u32[]{:S(2)}) collective-permute-start(bf16[1024,512]{1,0:T(8,128)(2,1)} %refs_9_.1), channel_id=1, source_target_pairs={{0,128},{128,256},{256,384},{384,0},{1,129},{129,257},{257,385},{3... | collective-permute-start | bytes 3145736 | tf_op jit(solution)/shard_map/ppermute | solution.py:27
  17.2 3.4 %collective-permute-start.11 = (bf16[1024,512]{1,0:T(8,128)(2,1)}, bf16[1024,512]{1,0:T(8,128)(2,1)S(1)}, u32[]{:S(2)}, u32[]{:S(2)}) collective-permute-start(bf16[1024,512]{1,0:T(8,128)(2,1)} %refs_9_.1), channel_id=1, source_target_pairs={{0,384},{128,0},{256,128},{384,256},{1,385},{129,1},{257,129},{385... | collective-permute-start | bytes 3145736 | tf_op jit(solution)/shard_map/ppermute | solution.py:27
  20.6 21.4 %collective-permute-done.9.refs_11_ = bf16[1024,512]{1,0:T(8,128)(2,1)S(1)} collective-permute-done((bf16[1024,512]{1,0:T(8,128)(2,1)}, bf16[1024,512]{1,0:T(8,128)(2,1)S(1)}, u32[]{:S(2)}, u32[]{:S(2)}) %collective-permute-start.9) | collective-permute-done | bytes 1048608 | tf_op jit(solution)/shard_map/ppermute | solution.py:27
  42.0 1.6 collective-permute-done.11.refs_13_
  43.6 1.2 broadcast_select_fusion
  44.9 4.6 %collective-permute-start.13 = (bf16[1024,512]{1,0:T(8,128)(2,1)}, bf16[1024,512]{1,0:T(8,128)(2,1)}, u32[]{:S(2)}, u32[]{:S(2)}) collective-permute-start(bf16[1024,512]{1,0:T(8,128)(2,1)} %broadcast_select_fusion), channel_id=1, source_target_pairs={{0,128},{1,385},{128,256},{129,1},{256,384},{257,129},{384,0},{385... | collective-permute-start | bytes 3145736 | tf_op jit(solution)/shard_map/ppermute | solution.py:32
  49.5 2.0 collective-permute-start
  51.4 0.6 pad_add_fusion.s_ref.refs_0_
  52.1 0.6 collective-permute-done.other_ref
  52.7 0.0 all-to-all-done.kv_ref
  52.7 0.7 copy-done.15
  53.4 1.0 copy-done.2
  54.3 7.1 %attend.1.refs_1_ = bf16[2,64,1024]{2,1,0:T(8,128)(2,1)} custom-call(s32[4]{0:T(128)} %pad_add_fusion.s_ref.refs_0_, s32[2]{0:T(128)} %cache_ref.1, s32[64]{0:T(128)} %length_ref.1, bf16[128,1024]{1,0:T(8,128)(2,1)} %mine_ref.1, bf16[64,1024]{1,0:T(8,128)(2,1)} %copy-done.15, bf16[16,2,128,128]{3,2,1,0:T(8,128)(2,1)} %copy-done.2, bf16[128,1024]{1,0:T(8,128)(2,1)} %dk_ref.1, ...), custom_call_target="tpu_custom_call" | custom-call | tf_op jit(solution)/shard_map/attend/pallas_call | solution.py:85
  61.5 5.1 %collective-permute-start.2 = (bf16[2,64,1024]{2,1,0:T(8,128)(2,1)}, bf16[2,64,1024]{2,1,0:T(8,128)(2,1)S(1)}, u32[]{:S(2)}, u32[]{:S(2)}) collective-permute-start(bf16[2,64,1024]{2,1,0:T(8,128)(2,1)} %attend.1.refs_1_), channel_id=1, source_target_pairs={{0,112},{16,0},{32,16},{48,32},{64,48},{80,64},{96,80},{112,96},{1... | collective-permute-start | bytes 786440 | tf_op jit(solution)/shard_map/ppermute | solution.py:27
  66.5 1.9 collective-permute-start.1
  68.5 3.9 %collective-permute-done.2.refs_3_ = bf16[2,64,1024]{2,1,0:T(8,128)(2,1)S(1)} collective-permute-done((bf16[2,64,1024]{2,1,0:T(8,128)(2,1)}, bf16[2,64,1024]{2,1,0:T(8,128)(2,1)S(1)}, u32[]{:S(2)}, u32[]{:S(2)}) %collective-permute-start.2) | collective-permute-done | bytes 262176 | tf_op jit(solution)/shard_map/ppermute | solution.py:27
  72.4 5.2 %collective-permute-start.4 = (bf16[2,64,1024]{2,1,0:T(8,128)(2,1)S(1)}, bf16[2,64,1024]{2,1,0:T(8,128)(2,1)S(1)}, u32[]{:S(2)}, u32[]{:S(2)}) collective-permute-start(bf16[2,64,1024]{2,1,0:T(8,128)(2,1)S(1)} %collective-permute-done.2.refs_3_), channel_id=1, source_target_pairs={{0,112},{16,0},{32,16},{48,32},{64,48},{80,64},{96,80},{112,96},{1... | collective-permute-start | bytes 786440 | tf_op jit(solution)/shard_map/ppermute | solution.py:27
  77.6 0.0 collective-permute-done.1.refs_2_
  77.6 1.9 collective-permute-start.3
  79.5 3.2 %collective-permute-start.8 = (bf16[1024,512]{1,0:T(8,128)(2,1)}, bf16[1024,512]{1,0:T(8,128)(2,1)S(1)}, u32[]{:S(2)}, u32[]{:S(2)}) collective-permute-start(bf16[1024,512]{1,0:T(8,128)(2,1)} %refs_9_.1), channel_id=1, source_target_pairs={{0,1},{1,0},{2,3},{3,2},{4,5},{5,4},{6,7},{7,6},{8,9},{9,8},{10,11... | collective-permute-start | bytes 3145736 | tf_op jit(solution)/shard_map/ppermute | solution.py:27
  82.7 1.9 collective-permute-start.10
  84.7 0.0 collective-permute-done.13.refs_15_
  84.7 2.4 %collective-permute-start.12 = (bf16[1024,512]{1,0:T(8,128)(2,1)S(1)}, bf16[1024,512]{1,0:T(8,128)(2,1)S(1)}, u32[]{:S(2)}, u32[]{:S(2)}) collective-permute-start(bf16[1024,512]{1,0:T(8,128)(2,1)S(1)} %collective-permute-done.11.refs_13_), channel_id=1, source_target_pairs={{0,1},{1,0},{2,3},{3,2},{4,5},{5,4},{6,7},{7,6},{8,9},{9,8},{10,11... | collective-permute-start | bytes 3145736 | tf_op jit(solution)/shard_map/ppermute | solution.py:27
  87.1 0.0 collective-permute-done.4.refs_5_
  87.1 1.9 collective-permute-start.14
  89.0 0.0 collective-permute-done.3.refs_4_
  89.1 4.9 %collective-permute-start.6 = (bf16[2,64,1024]{2,1,0:T(8,128)(2,1)S(1)}, bf16[2,64,1024]{2,1,0:T(8,128)(2,1)S(1)}, u32[]{:S(2)}, u32[]{:S(2)}) collective-permute-start(bf16[2,64,1024]{2,1,0:T(8,128)(2,1)S(1)} %collective-permute-done.4.refs_5_), channel_id=1, source_target_pairs={{0,112},{16,0},{32,16},{48,32},{64,48},{80,64},{96,80},{112,96},{1... | collective-permute-start | bytes 786440 | tf_op jit(solution)/shard_map/ppermute | solution.py:27
  93.9 5.1 %collective-permute-done.6.refs_7_ = bf16[2,64,1024]{2,1,0:T(8,128)(2,1)S(1)} collective-permute-done((bf16[2,64,1024]{2,1,0:T(8,128)(2,1)S(1)}, bf16[2,64,1024]{2,1,0:T(8,128)(2,1)S(1)}, u32[]{:S(2)}, u32[]{:S(2)}) %collective-permute-start.6) | collective-permute-done | bytes 262176 | tf_op jit(solution)/shard_map/ppermute | solution.py:27
  99.1 1.9 collective-permute-start.5
  101.0 8.7 %collective-permute-done.5.refs_6_ = bf16[2,64,1024]{2,1,0:T(8,128)(2,1)S(1)} collective-permute-done((bf16[2,64,1024]{2,1,0:T(8,128)(2,1)S(1)}, bf16[2,64,1024]{2,1,0:T(8,128)(2,1)S(1)}, u32[]{:S(2)}, u32[]{:S(2)}) %collective-permute-start.5) | collective-permute-done | bytes 262176 | tf_op jit(solution)/shard_map/ppermute | solution.py:27
  109.7 3.1 %collective-permute-start.7 = (bf16[2,64,1024]{2,1,0:T(8,128)(2,1)S(1)}, bf16[2,64,1024]{2,1,0:T(8,128)(2,1)S(1)}, u32[]{:S(2)}, u32[]{:S(2)}) collective-permute-start(bf16[2,64,1024]{2,1,0:T(8,128)(2,1)S(1)} %broadcast_select_fusion.1), channel_id=1, source_target_pairs={{0,16},{1,113},{16,32},{17,1},{32,48},{33,17},{48,64},{49,33},{64,... | collective-permute-start | bytes 786440 | tf_op jit(solution)/shard_map/ppermute | solution.py:32
  112.8 0.0 collective-permute-done.8.refs_10_
  112.9 0.0 collective-permute-done.10.refs_12_
  112.9 0.0 copy-start.4
  112.9 0.0 collective-permute-done.12.refs_14_
  112.9 1.0 copy-done.4
  113.9 3.0 %collective-permute-done.7.refs_8_ = bf16[2,64,1024]{2,1,0:T(8,128)(2,1)S(1)} collective-permute-done((bf16[2,64,1024]{2,1,0:T(8,128)(2,1)S(1)}, bf16[2,64,1024]{2,1,0:T(8,128)(2,1)S(1)}, u32[]{:S(2)}, u32[]{:S(2)}) %collective-permute-start.7) | collective-permute-done | bytes 262176 | tf_op jit(solution)/shard_map/ppermute | solution.py:32
  116.9 0.7 copy-done.14
  117.6 0.0 collective-permute-done.14.refs_16_
  117.6 1.0 copy-done.6
  118.6 0.6 broadcast_in_dim.3.refs_17_
  119.2 9.8 %project.1 = (bf16[4,8,32,1024]{3,2,1,0:T(8,128)(2,1)}, f32[8,128]{1,0:T(8,128)}) custom-call(s32[4]{0:T(128)} %pad_add_fusion.s_ref.refs_0_, bf16[2,64,1024]{2,1,0:T(8,128)(2,1)} %attend.1.refs_1_, bf16[2,64,1024]{2,1,0:T(8,128)(2,1)} %copy-done.11, bf16[2,64,1024]{2,1,0:T(8,128)(2,1)} %copy-done.10, bf16[2,64,1024]{2,1,0:T(8,128)(2,1)} %copy-done.13, ...), custom_call_target="tpu_custom_call" | custom-call | tf_op jit(solution)/shard_map/project/pallas_call | solution.py:130
  129.0 51.7 %all_to_all.15 = bf16[32,32,1024]{2,1,0:T(8,128)(2,1)} all-to-all(bf16[32,32,1024]{2,1,0:T(8,128)(2,1)} %bitcast.9), channel_id=1, replica_groups=mesh['x'=4,'y'=8,'z'=8,'c'=2] {'x','z'}, dimensions={0} | all-to-all | bytes 4194304 | tf_op jit(solution)/shard_map/all_to_all | solution.py:205
  180.7 3.0 %place.1 = bf16[16,32,384]{2,1,0:T(8,128)(2,1)} custom-call(s32[4]{0:T(128)} %pad_add_fusion.s_ref.refs_0_, s32[64]{0:T(128)} %length_ref.1, s32[64]{0:T(128)} %group_ref.1, s32[64]{0:T(128)} %first_ref.1, bf16[4,8,32,1024]{3,2,1,0:T(8,128)(2,1)} %bitcast.7), custom_call_target="tpu_custom_call" | custom-call | tf_op jit(solution)/shard_map/place/pallas_call | solution.py:169
  183.7 28.0 %all_to_all.16.i_ref = bf16[16,32,384]{2,1,0:T(8,128)(2,1)} all-to-all(bf16[16,32,384]{2,1,0:T(8,128)(2,1)} %place.1), channel_id=1, replica_groups=mesh['x'=4,'y'=8,'z'=8,'c'=2] {'z','c'}, dimensions={0} | all-to-all | bytes 786432 | tf_op jit(solution)/shard_map/all_to_all | solution.py:205
  211.7 1.9 finish.1
  (28 shorter events, 0.1 us)
Async XLA Ops:
  2.1 50.6 %all-to-all-start = ((bf16[16,2,128,128]{3,2,1,0:T(8,128)(2,1)}), bf16[16,2,128,128]{3,2,1,0:T(8,128)(2,1)S(1)}, u32[]{:S(2)}, u32[]{:S(2)}) async-start(bf16[16,2,128,128]{3,2,1,0:T(8,128)(2,1)} %bitcast.8), calls=%async_computation | async-start | bytes 2097152 | tf_op jit(solution)/shard_map/all_to_all | solution.py:205
  13.9 35.5 %copy-start.9 = (bf16[128,1024]{1,0:T(8,128)(2,1)S(1)}, bf16[128,1024]{1,0:T(8,128)(2,1)}, u32[]{:S(2)}) copy-start(bf16[128,1024]{1,0:T(8,128)(2,1)} %mine_ref.1) | copy-start | bytes 786436
  13.9 28.1 %collective-permute-start.9 = (bf16[1024,512]{1,0:T(8,128)(2,1)}, bf16[1024,512]{1,0:T(8,128)(2,1)S(1)}, u32[]{:S(2)}, u32[]{:S(2)}) collective-permute-start(bf16[1024,512]{1,0:T(8,128)(2,1)} %refs_9_.1), channel_id=1, source_target_pairs={{0,128},{128,256},{256,384},{384,0},{1,129},{129,257},{257,385},{3... | collective-permute-start | bytes 3145736 | tf_op jit(solution)/shard_map/ppermute | solution.py:27
  17.2 26.4 %collective-permute-start.11 = (bf16[1024,512]{1,0:T(8,128)(2,1)}, bf16[1024,512]{1,0:T(8,128)(2,1)S(1)}, u32[]{:S(2)}, u32[]{:S(2)}) collective-permute-start(bf16[1024,512]{1,0:T(8,128)(2,1)} %refs_9_.1), channel_id=1, source_target_pairs={{0,384},{128,0},{256,128},{384,256},{1,385},{129,1},{257,129},{385... | collective-permute-start | bytes 3145736 | tf_op jit(solution)/shard_map/ppermute | solution.py:27
  42.0 40.7 %copy-start = (bf16[1024,512]{1,0:T(8,128)(2,1)}, bf16[1024,512]{1,0:T(8,128)(2,1)S(1)}, u32[]{:S(2)}) copy-start(bf16[1024,512]{1,0:T(8,128)(2,1)S(1)} %collective-permute-done.9.refs_11_) | copy-start | bytes 3145732
  43.6 41.0 %copy-start.1 = (bf16[1024,512]{1,0:T(8,128)(2,1)}, bf16[1024,512]{1,0:T(8,128)(2,1)S(1)}, u32[]{:S(2)}) copy-start(bf16[1024,512]{1,0:T(8,128)(2,1)S(1)} %collective-permute-done.11.refs_13_) | copy-start | bytes 3145732
  44.9 39.8 %collective-permute-start.13 = (bf16[1024,512]{1,0:T(8,128)(2,1)}, bf16[1024,512]{1,0:T(8,128)(2,1)}, u32[]{:S(2)}, u32[]{:S(2)}) collective-permute-start(bf16[1024,512]{1,0:T(8,128)(2,1)} %broadcast_select_fusion), channel_id=1, source_target_pairs={{0,128},{1,385},{128,256},{129,1},{256,384},{257,129},{384,0},{385... | collective-permute-start | bytes 3145736 | tf_op jit(solution)/shard_map/ppermute | solution.py:32
  49.5 3.2 %collective-permute-start = (bf16[64,1024]{1,0:T(8,128)(2,1)S(1)}, bf16[64,1024]{1,0:T(8,128)(2,1)S(1)}, u32[]{:S(2)}, u32[]{:S(2)}) collective-permute-start(bf16[64,1024]{1,0:T(8,128)(2,1)S(1)} %constant_dynamic-slice_fusion), channel_id=1, source_target_pairs={{0,1},{1,0},{2,3},{3,2},{4,5},{5,4},{6,7},{7,6},{8,9},{9,8},{10,11... | collective-permute-start | bytes 393224 | tf_op jit(solution)/shard_map/ppermute | solution.py:27
  52.7 0.7 copy-start.15
  53.4 1.0 copy-start.2
  61.5 10.9 %collective-permute-start.2 = (bf16[2,64,1024]{2,1,0:T(8,128)(2,1)}, bf16[2,64,1024]{2,1,0:T(8,128)(2,1)S(1)}, u32[]{:S(2)}, u32[]{:S(2)}) collective-permute-start(bf16[2,64,1024]{2,1,0:T(8,128)(2,1)} %attend.1.refs_1_), channel_id=1, source_target_pairs={{0,112},{16,0},{32,16},{48,32},{64,48},{80,64},{96,80},{112,96},{1... | collective-permute-start | bytes 786440 | tf_op jit(solution)/shard_map/ppermute | solution.py:27
  66.5 11.0 %collective-permute-start.1 = (bf16[2,64,1024]{2,1,0:T(8,128)(2,1)}, bf16[2,64,1024]{2,1,0:T(8,128)(2,1)S(1)}, u32[]{:S(2)}, u32[]{:S(2)}) collective-permute-start(bf16[2,64,1024]{2,1,0:T(8,128)(2,1)} %attend.1.refs_1_), channel_id=1, source_target_pairs={{0,16},{16,32},{32,48},{48,64},{64,80},{80,96},{96,112},{112,0},{1... | collective-permute-start | bytes 786440 | tf_op jit(solution)/shard_map/ppermute | solution.py:27
  72.4 26.7 %copy-start.10 = (bf16[2,64,1024]{2,1,0:T(8,128)(2,1)}, bf16[2,64,1024]{2,1,0:T(8,128)(2,1)S(1)}, u32[]{:S(2)}) copy-start(bf16[2,64,1024]{2,1,0:T(8,128)(2,1)S(1)} %collective-permute-done.2.refs_3_) | copy-start | bytes 786436
  72.4 14.7 %collective-permute-start.4 = (bf16[2,64,1024]{2,1,0:T(8,128)(2,1)S(1)}, bf16[2,64,1024]{2,1,0:T(8,128)(2,1)S(1)}, u32[]{:S(2)}, u32[]{:S(2)}) collective-permute-start(bf16[2,64,1024]{2,1,0:T(8,128)(2,1)S(1)} %collective-permute-done.2.refs_3_), channel_id=1, source_target_pairs={{0,112},{16,0},{32,16},{48,32},{64,48},{80,64},{96,80},{112,96},{1... | collective-permute-start | bytes 786440 | tf_op jit(solution)/shard_map/ppermute | solution.py:27
  77.6 23.4 %copy-start.11 = (bf16[2,64,1024]{2,1,0:T(8,128)(2,1)}, bf16[2,64,1024]{2,1,0:T(8,128)(2,1)S(1)}, u32[]{:S(2)}) copy-start(bf16[2,64,1024]{2,1,0:T(8,128)(2,1)S(1)} %collective-permute-done.1.refs_2_) | copy-start | bytes 786436
  77.6 11.4 %collective-permute-start.3 = (bf16[2,64,1024]{2,1,0:T(8,128)(2,1)S(1)}, bf16[2,64,1024]{2,1,0:T(8,128)(2,1)S(1)}, u32[]{:S(2)}, u32[]{:S(2)}) collective-permute-start(bf16[2,64,1024]{2,1,0:T(8,128)(2,1)S(1)} %collective-permute-done.1.refs_2_), channel_id=1, source_target_pairs={{0,16},{16,32},{32,48},{48,64},{64,80},{80,96},{96,112},{112,0},{1... | collective-permute-start | bytes 786440 | tf_op jit(solution)/shard_map/ppermute | solution.py:27
  79.5 33.3 %collective-permute-start.8 = (bf16[1024,512]{1,0:T(8,128)(2,1)}, bf16[1024,512]{1,0:T(8,128)(2,1)S(1)}, u32[]{:S(2)}, u32[]{:S(2)}) collective-permute-start(bf16[1024,512]{1,0:T(8,128)(2,1)} %refs_9_.1), channel_id=1, source_target_pairs={{0,1},{1,0},{2,3},{3,2},{4,5},{5,4},{6,7},{7,6},{8,9},{9,8},{10,11... | collective-permute-start | bytes 3145736 | tf_op jit(solution)/shard_map/ppermute | solution.py:27
  82.7 30.1 %collective-permute-start.10 = (bf16[1024,512]{1,0:T(8,128)(2,1)S(1)}, bf16[1024,512]{1,0:T(8,128)(2,1)S(1)}, u32[]{:S(2)}, u32[]{:S(2)}) collective-permute-start(bf16[1024,512]{1,0:T(8,128)(2,1)S(1)} %collective-permute-done.9.refs_11_), channel_id=1, source_target_pairs={{0,1},{1,0},{2,3},{3,2},{4,5},{5,4},{6,7},{7,6},{8,9},{9,8},{10,11... | collective-permute-start | bytes 3145736 | tf_op jit(solution)/shard_map/ppermute | solution.py:27
  84.7 28.2 %collective-permute-start.12 = (bf16[1024,512]{1,0:T(8,128)(2,1)S(1)}, bf16[1024,512]{1,0:T(8,128)(2,1)S(1)}, u32[]{:S(2)}, u32[]{:S(2)}) collective-permute-start(bf16[1024,512]{1,0:T(8,128)(2,1)S(1)} %collective-permute-done.11.refs_13_), channel_id=1, source_target_pairs={{0,1},{1,0},{2,3},{3,2},{4,5},{5,4},{6,7},{7,6},{8,9},{9,8},{10,11... | collective-permute-start | bytes 3145736 | tf_op jit(solution)/shard_map/ppermute | solution.py:27
  87.1 13.9 %copy-start.12 = (bf16[2,64,1024]{2,1,0:T(8,128)(2,1)}, bf16[2,64,1024]{2,1,0:T(8,128)(2,1)S(1)}, u32[]{:S(2)}) copy-start(bf16[2,64,1024]{2,1,0:T(8,128)(2,1)S(1)} %collective-permute-done.4.refs_5_) | copy-start | bytes 786436
  87.1 30.4 %collective-permute-start.14 = (bf16[1024,512]{1,0:T(8,128)(2,1)}, bf16[1024,512]{1,0:T(8,128)(2,1)S(1)}, u32[]{:S(2)}, u32[]{:S(2)}) collective-permute-start(bf16[1024,512]{1,0:T(8,128)(2,1)} %collective-permute-done.13.refs_15_), channel_id=1, source_target_pairs={{0,1},{1,0},{2,3},{3,2},{4,5},{5,4},{6,7},{7,6},{8,9},{9,8},{10,11... | collective-permute-start | bytes 3145736 | tf_op jit(solution)/shard_map/ppermute | solution.py:27
  89.1 12.0 %copy-start.13 = (bf16[2,64,1024]{2,1,0:T(8,128)(2,1)}, bf16[2,64,1024]{2,1,0:T(8,128)(2,1)S(1)}, u32[]{:S(2)}) copy-start(bf16[2,64,1024]{2,1,0:T(8,128)(2,1)S(1)} %collective-permute-done.3.refs_4_) | copy-start | bytes 786436
  89.1 10.0 %collective-permute-start.6 = (bf16[2,64,1024]{2,1,0:T(8,128)(2,1)S(1)}, bf16[2,64,1024]{2,1,0:T(8,128)(2,1)S(1)}, u32[]{:S(2)}, u32[]{:S(2)}) collective-permute-start(bf16[2,64,1024]{2,1,0:T(8,128)(2,1)S(1)} %collective-permute-done.4.refs_5_), channel_id=1, source_target_pairs={{0,112},{16,0},{32,16},{48,32},{64,48},{80,64},{96,80},{112,96},{1... | collective-permute-start | bytes 786440 | tf_op jit(solution)/shard_map/ppermute | solution.py:27
  99.1 20.1 %copy-start.7 = (bf16[2,64,1024]{2,1,0:T(8,128)(2,1)}, bf16[2,64,1024]{2,1,0:T(8,128)(2,1)S(1)}, u32[]{:S(2)}) copy-start(bf16[2,64,1024]{2,1,0:T(8,128)(2,1)S(1)} %collective-permute-done.6.refs_7_) | copy-start | bytes 786436
  99.1 10.6 %collective-permute-start.5 = (bf16[2,64,1024]{2,1,0:T(8,128)(2,1)S(1)}, bf16[2,64,1024]{2,1,0:T(8,128)(2,1)S(1)}, u32[]{:S(2)}, u32[]{:S(2)}) collective-permute-start(bf16[2,64,1024]{2,1,0:T(8,128)(2,1)S(1)} %collective-permute-done.3.refs_4_), channel_id=1, source_target_pairs={{0,16},{16,32},{32,48},{48,64},{64,80},{80,96},{96,112},{112,0},{1... | collective-permute-start | bytes 786440 | tf_op jit(solution)/shard_map/ppermute | solution.py:27
  109.7 7.9 %copy-start.8 = (bf16[2,64,1024]{2,1,0:T(8,128)(2,1)}, bf16[2,64,1024]{2,1,0:T(8,128)(2,1)S(1)}, u32[]{:S(2)}) copy-start(bf16[2,64,1024]{2,1,0:T(8,128)(2,1)S(1)} %collective-permute-done.5.refs_6_) | copy-start | bytes 786436
  109.7 7.1 %collective-permute-start.7 = (bf16[2,64,1024]{2,1,0:T(8,128)(2,1)S(1)}, bf16[2,64,1024]{2,1,0:T(8,128)(2,1)S(1)}, u32[]{:S(2)}, u32[]{:S(2)}) collective-permute-start(bf16[2,64,1024]{2,1,0:T(8,128)(2,1)S(1)} %broadcast_select_fusion.1), channel_id=1, source_target_pairs={{0,16},{1,113},{16,32},{17,1},{32,48},{33,17},{48,64},{49,33},{64,... | collective-permute-start | bytes 786440 | tf_op jit(solution)/shard_map/ppermute | solution.py:32
  112.8 6.3 %copy-start.3 = (bf16[1024,512]{1,0:T(8,128)(2,1)}, bf16[1024,512]{1,0:T(8,128)(2,1)S(1)}, u32[]{:S(2)}) copy-start(bf16[1024,512]{1,0:T(8,128)(2,1)S(1)} %collective-permute-done.8.refs_10_) | copy-start | bytes 3145732
  112.9 1.0 copy-start.4
  113.9 3.0 %copy-start.5 = (bf16[1024,512]{1,0:T(8,128)(2,1)}, bf16[1024,512]{1,0:T(8,128)(2,1)S(1)}, u32[]{:S(2)}) copy-start(bf16[1024,512]{1,0:T(8,128)(2,1)S(1)} %collective-permute-done.12.refs_14_) | copy-start | bytes 3145732
  116.9 0.7 copy-start.14
  117.6 1.0 copy-start.6
